TPU v7x, 256 devices: a whole 4x4x8 slice. The times are simulated.
256 devices in a mesh: dp: 128 (over z, x, y), rep: 2 (over core).
Axes of the slice: x: 4, y: 4, z: 8, core: 2. Of those that a mesh axis runs over, the one named last changes fastest.
Arguments:
- ids: int32 [65536], P(('dp', 'rep')), may hold values from 0 to 65520
- counts: int32 [256], P(('dp', 'rep')), may hold values from 1 to 256, as said below
- hash_scale: int32 [512], replicated, may hold values from 1 to 32767
- hash_shift: int32 [512], replicated, may hold values from 0 to 65520
- w_code: bfloat16 [512, 1024], replicated, may hold values from -0.25 to 0.25
- norm_gain: float32 [1024], replicated, may hold values from 0.5 to 1.5
- norm_bias: float32 [1024], replicated, may hold values from -3 to 3
- w_out: bfloat16 [1024, 128], replicated, may hold values from -0.1875 to 0.1875
- out_bias: float32 [128], replicated, may hold values from -3 to 3
- cotangent: bfloat16 [65536, 128], P(('dp', 'rep')), may hold values from -6 to 6
Outputs:
- embeddings: bfloat16 [65536, 128], P(('dp', 'rep'))
- grad_code_t: float32 [1024, 512], P(('dp', 'rep'))
- grad_out: float32 [1024, 128], P(('dp', 'rep'))
- grad_gain: float32 [1024], replicated
- grad_bias: float32 [1024], replicated
Inputs may be any that keep to these rules, and one draw needn't show every extreme that they name: Each device has 1 to 256 live slots, the first ones of its slots; the counts of the devices of one rep index sum to exactly 8192, and in each such group one device has exactly 256.
All inputs are finite; a program needn't handle non-finite values.
Results may differ from a plain program's by a relative error of at most 0.006.
Values may be sent and summed in bfloat16 or wider, within the bound.
A program may use at most 64 MiB of HBM per device.

v0:
```python
import jax
import jax.numpy as jnp
from jax import lax
from jax.sharding import Mesh
from jax.sharding import PartitionSpec as P

BLOCK = 256
DP_REP = ("dp_0", "dp_1", "dp_2", "rep")


modulus = 65521
epsilon = 1e-05


def sent_to_all(shard, axis):
    copies = jnp.broadcast_to(shard, (lax.axis_size(axis), *shard.shape))
    return lax.all_to_all(copies, axis, split_axis=0, concat_axis=0, tiled=True)


def over_copies(shard, axis):
    everything = sent_to_all(shard, axis)
    return jnp.sum(everything, axis=0)


def over_axes(shard, axes):
    far, near = axes
    return over_copies(over_copies(shard, near), far)


def in_one(arrays, axis):
    ends = [0]
    for a in arrays:
        ends.append(ends[-1] + a.size)
    subtotal = over_axes(jnp.concatenate([a.ravel() for a in arrays]), axis)
    return tuple((subtotal[b:e].reshape(a.shape) for a, b, e in zip(arrays, ends, ends[1:])))


def split_up(shard, dim, count):
    lengths = shard.shape
    pieces = shard.reshape(*lengths[:dim], count, lengths[dim] // count, *lengths[dim + 1 :])
    return jnp.moveaxis(pieces, dim, 0)


def sent_and_summed(shard, axis, dim):
    pieces = split_up(shard, dim, lax.axis_size(axis))
    arrived = lax.all_to_all(pieces, axis, split_axis=0, concat_axis=0, tiled=True)
    return arrived.astype(jnp.float32).sum(axis=0)


def summed_rows(shard, axes, dim):
    far, near = axes
    pieces = split_up(shard, dim, lax.axis_size(far))
    nearer = sent_and_summed(pieces, near, dim + 1)
    arrived = lax.all_to_all(
        nearer.astype(jnp.bfloat16), far, split_axis=0, concat_axis=0, tiled=True
    )
    return arrived.astype(jnp.float32).sum(axis=0)


def side_by_side(arrays, axis, dim, along):
    ends, at = ([], 0)
    for a in arrays[:-1]:
        at += a.shape[along]
        ends.append(at)
    both = jnp.concatenate(arrays, axis=along)
    return tuple(jnp.split(summed_rows(both, axis, dim), ends, axis=along))


def hashed(ident, hash_scale, hash_shift):
    resid = ident % modulus
    bucket = (hash_scale[None, :] * resid[:, None] + hash_shift[None, :]) % modulus
    return (bucket.astype(jnp.float32) * (2.0 / (modulus - 1)) - 1.0).astype(jnp.bfloat16)


def mish_parts(gated):
    softer = jax.nn.softplus(gated)
    tangent = jnp.tanh(softer)
    return (gated * tangent, tangent + gated * (1.0 - tangent * tangent) * jax.nn.sigmoid(gated))


def train_rows(
    code_rows,
    cot_rows,
    live_count,
    row_ids,
    hash_scale,
    hash_shift,
    w_code,
    norm_gain,
    norm_bias,
    w_out,
    out_bias,
):
    row_count = code_rows.shape[0]
    hidden = w_code.shape[1]
    width = w_out.shape[1]
    live_flags = jnp.arange(row_count, dtype=jnp.int32) < live_count
    block_total = (live_count + BLOCK - 1) // BLOCK
    zero_row = jnp.zeros((hidden,), jnp.float32)

    def first_pass(block_index, state_carry):
        stored, sum_hidden, sum_square = state_carry
        keep_rows = live_flags[:, None]
        preact = jnp.dot(code_rows, w_code, preferred_element_type=jnp.float32)
        masked = jnp.where(keep_rows, preact, 0.0)
        stored = preact
        return (stored, sum_hidden + masked.sum(0), sum_square + (masked * masked).sum(0))

    stored, sum_hidden, sum_square = lax.fori_loop(
        0,
        block_total,
        first_pass,
        (jnp.zeros((row_count, hidden), jnp.float32), zero_row, zero_row),
    )
    sum_hidden, sum_square, total = in_one(
        (sum_hidden, sum_square, live_count.astype(jnp.float32)),
        (("dp_0", "dp_1"), ("dp_2", "rep")),
    )
    feature_mean = sum_hidden / total
    inv_std = lax.rsqrt(sum_square / total - feature_mean * feature_mean + epsilon)
    loss_scale = lax.rsqrt(total)

    def second_pass(block_index, state_carry):
        stored, dvalue_rows, embedded, grad_gain, grad_bias, grad_out = state_carry
        keep_rows = live_flags[:, None]
        normed = (stored - feature_mean) * inv_std
        act_full, mish_slope = mish_parts(normed * norm_gain + norm_bias)
        activation = act_full.astype(jnp.bfloat16)
        out_rows = jnp.dot(activation, w_out, preferred_element_type=jnp.float32) + out_bias
        out_rows = jnp.where(keep_rows, out_rows, 0.0).astype(jnp.bfloat16)
        delta_rows = jnp.where(keep_rows, cot_rows.astype(jnp.float32) * loss_scale, 0.0).astype(
            jnp.bfloat16
        )
        grad_act = lax.dot_general(
            delta_rows, w_out, (((1,), (1,)), ((), ())), preferred_element_type=jnp.float32
        )
        dvalue = grad_act * mish_slope
        stored = normed
        dvalue_rows = dvalue
        embedded = out_rows
        out_part = lax.dot_general(
            activation, delta_rows, (((0,), (0,)), ((), ())), preferred_element_type=jnp.float32
        )
        return (
            stored,
            dvalue_rows,
            embedded,
            grad_gain + (dvalue * normed).sum(0),
            grad_bias + dvalue.sum(0),
            grad_out + out_part,
        )

    start_state = (
        stored,
        jnp.zeros((row_count, hidden), jnp.float32),
        jnp.zeros((row_count, width), jnp.bfloat16),
        zero_row,
        zero_row,
        jnp.zeros((hidden, width), jnp.float32),
    )
    stored, dvalue_rows, embedded, grad_gain, grad_bias, grad_out = lax.fori_loop(
        0, block_total, second_pass, start_state
    )
    grad_gain, grad_bias = in_one((grad_gain, grad_bias), (("dp_0", "dp_1"), ("dp_2", "rep")))

    def signal_block():
        keep_rows = live_flags[:, None]
        dpre = norm_gain * inv_std * (dvalue_rows - grad_bias / total - stored * grad_gain / total)
        return jnp.where(keep_rows, dpre, 0.0).astype(jnp.bfloat16)

    def third_pass(block_index, grad_code):
        return grad_code + lax.dot_general(
            signal_block(), code_rows, (((0,), (0,)), ((), ())), preferred_element_type=jnp.float32
        )

    grad_code = lax.fori_loop(
        0, block_total, third_pass, jnp.zeros((hidden, w_code.shape[0]), jnp.float32)
    )
    code_share, out_share = side_by_side(
        (grad_code.astype(jnp.bfloat16), grad_out.astype(jnp.bfloat16)),
        (("dp_0", "dp_1"), ("dp_2", "rep")),
        0,
        1,
    )
    return (embedded, code_share, out_share, grad_gain, grad_bias)


def per_device(
    ids, counts, hash_scale, hash_shift, w_code, norm_gain, norm_bias, w_out, out_bias, cotangent
):
    live_count = counts[0]
    weights = (w_code, norm_gain, norm_bias, w_out, out_bias)
    code_rows = hashed(ids, hash_scale, hash_shift)
    embedded, code_share, out_share, grad_gain, grad_bias = train_rows(
        code_rows, cotangent, live_count, ids, hash_scale, hash_shift, *weights
    )
    return (embedded, code_share, out_share, grad_gain, grad_bias)


def solution(mesh):
    finer = Mesh(mesh.devices.reshape(8, 4, 4, mesh.shape["rep"]), ("dp_0", "dp_1", "dp_2", "rep"))
    return jax.shard_map(
        per_device,
        mesh=finer,
        in_specs=(P(DP_REP), P(DP_REP), P(), P(), P(), P(), P(), P(), P(), P(DP_REP, None)),
        out_specs=(P(DP_REP, None), P(DP_REP, None), P(DP_REP, None), P(), P()),
        check_vma=False,
    )
```

profile of v0, /device:TPU:1, one launch (start us, length us, event | category | flops | bytes accessed | tf_op | source)
XLA Modules:
  0.0 123.4 jit_solution(15541596397151485691)
XLA Ops:
  0.6 0.0 copy-start
  1.4 0.7 and_select_fusion
  2.1 0.0 copy-done
  2.1 1.4 %multiply_reduce_fusion.1 = (f32[1024]{0:T(1024)S(1)}, f32[1024]{0:T(1024)S(1)}, f32[256,1024]{1,0:T(8,128)S(1)}) fusion(pred[256]{0:T(512)(128)(4,1)S(1)} %iota_compare_fusion.1, bf16[512,1024]{1,0:T(8,128)(2,1)S(1)} %copy-done, s32[512]{0:T(512)} %param.19, s32[256]{0:T(256)S(1)} %and_select_fusion, s32[512]{0:T(512)} %param.18), kind=kOutput, calls=%fused_computation.19 | convolution fusion | flops 271054848 | bytes 2110720 | tf_op jit(solution)/shard_map/while/body/dot_general | solution.py:104
  3.6 1.1 broadcast.47.clone
  4.7 1.0 while.53
  4.7 1.0 copy.48
  5.7 0.0 copy-start.6
  5.8 10.8 %all_to_all.36 = f32[8,1,2049]{2,1,0:T(1,128)S(1)} all-to-all(f32[8,1,2049]{2,1,0:T(1,128)S(1)} %broadcast_in_dim.88), channel_id=1, replica_groups=mesh['dp_0'=8,'dp_1'=4,'dp_2'=4,'rep'=2] {'dp_2','rep'}, dimensions={0} | all-to-all | bytes 131136 | tf_op jit(solution)/shard_map/all_to_all | solution.py:17
  16.5 0.1 reduce_sum.103
  16.6 0.9 broadcast_in_dim.89
  17.5 11.0 %all-to-all-start.1 = ((f32[32,1,2049]{2,1,0:T(1,128)}), f32[32,1,2049]{2,1,0:T(1,128)S(1)}, u32[]{:S(2)}, u32[]{:S(2)}) async-start(f32[32,1,2049]{2,1,0:T(1,128)} %broadcast_in_dim.89), calls=%async_computation.1 | async-start | bytes 557056 | tf_op jit(solution)/shard_map/all_to_all | solution.py:17
  28.5 11.4 %all-to-all-done.1 = f32[32,1,2049]{2,1,0:T(1,128)S(1)} async-done(((f32[32,1,2049]{2,1,0:T(1,128)}), f32[32,1,2049]{2,1,0:T(1,128)S(1)}, u32[]{:S(2)}, u32[]{:S(2)}) %all-to-all-start.1) | async-done | bytes 262304 | tf_op jit(solution)/shard_map/all_to_all | solution.py:17
  39.9 0.2 reduce_sum.104
  40.1 0.5 slice.21
  41.2 0.0 copy-done.4
  41.2 0.6 fusion.37
  41.8 0.6 broadcast_in_dim.86
  42.4 1.1 broadcast.47
  43.5 0.0 copy-done.1
  43.6 5.0 %while.55 = (s32[]{:T(128)}, f32[256,1024]{1,0:T(8,128)S(1)}, f32[256,1024]{1,0:T(8,128)}, bf16[256,128]{1,0:T(8,128)(2,1)}, f32[1024]{0:T(1024)S(1)}, /*index=5...) while((s32[]{:T(128)}, f32[256,1024]{1,0:T(8,128)S(1)}, ...), condition=%wide.region_9.10_spmd.clone, body=%wide.region_6.9_spmd.clone.sunk | while | flops 210206976 | bytes 7595697 | solution.py:161
  43.6 0.7 iota_compare_fusion.3
  44.2 0.8 multiply_convert_fusion.2
  45.0 0.9 fusion.55
  46.0 0.4 convolution_add_fusion.3
  46.4 2.2 %fusion.54 = (f32[1024]{0:T(1024)S(1)}, f32[1024]{0:T(1024)S(1)}, f32[256,1024]{1,0:T(8,128)}) fusion(f32[256,1024]{1,0:T(8,128)S(1)} %get-tuple-element.796, f32[1024]{0:T(1024)S(1)} %get-tuple-element.809, f32[1024]{0:T(1024)S(1)} %get-tuple-element.808, bf16[1024,128]{1,0:T(8,128)(2,1)S(1)} %get-tuple-element.807, ...), kind=kOutput, calls=%fused_computation.58.clone.1 | convolution fusion | flops 72480768 | bytes 2441476 | tf_op jit(solution)/shard_map/while/body/dot_general | solution.py:134
  48.6 0.0 copy-start.9
  48.7 9.7 %all_to_all.37 = f32[8,1,2048]{2,1,0:T(1,128)S(1)} all-to-all(f32[8,1,2048]{2,1,0:T(1,128)S(1)} %broadcast_in_dim.91), channel_id=1, replica_groups=mesh['dp_0'=8,'dp_1'=4,'dp_2'=4,'rep'=2] {'dp_2','rep'}, dimensions={0} | all-to-all | bytes 131072 | tf_op jit(solution)/shard_map/all_to_all | solution.py:17
  58.4 0.1 reduce_sum.105
  58.5 0.8 broadcast_in_dim.92
  59.3 3.9 %all-to-all-start.3 = ((f32[32,1,2048]{2,1,0:T(1,128)}), f32[32,1,2048]{2,1,0:T(1,128)S(1)}, u32[]{:S(2)}, u32[]{:S(2)}) async-start(f32[32,1,2048]{2,1,0:T(1,128)} %broadcast_in_dim.92), calls=%async_computation.3 | async-start | bytes 524288 | tf_op jit(solution)/shard_map/all_to_all | solution.py:17
  63.2 11.2 %all-to-all-done.3 = f32[32,1,2048]{2,1,0:T(1,128)S(1)} async-done(((f32[32,1,2048]{2,1,0:T(1,128)}), f32[32,1,2048]{2,1,0:T(1,128)S(1)}, u32[]{:S(2)}, u32[]{:S(2)}) %all-to-all-start.3) | async-done | bytes 262176 | tf_op jit(solution)/shard_map/all_to_all | solution.py:17
  74.4 0.2 reduce_sum.106
  74.6 1.1 broadcast_divide_fusion
  75.7 0.0 copy-done.9
  75.7 4.0 %fusion.11 = f32[1024,512]{1,0:T(8,128)} fusion(f32[256,1024]{1,0:T(8,128)S(1)} %get-tuple-element.437, f32[256,1024]{1,0:T(8,128)} %get-tuple-element.434, f32[]{:T(128)} %bitcast.2, f32[1024]{0:T(1024)S(1)} %get-tuple-element.546, f32[1024]{0:T(1024)S(1)} %get-tuple-element.542, f32[1024]{0:T(1024)S(1)} %get-tuple-element.540, ...), kind=kOutput, calls=%fused_computation.26 | convolution fusion | flops 271843328 | bytes 4211972 | tf_op jit(solution)/shard_map/while/body/dot_general | solution.py:172
  79.8 0.2 broadcast_in_dim.90
  80.0 2.2 %while.54 = (s32[]{:T(128)}, f32[1024,512]{1,0:T(8,128)S(1)}, s32[]{:T(128)}, f32[1024,512]{1,0:T(8,128)}, s32[]{:T(128)}) while((s32[]{:T(128)}, f32[1024,512]{1,0:T(8,128)S(1)}, s32[]{:T(128)}, f32[1024,512]{1,0:T(8,128)}, s32[]{:T(128)}) %tuple.98), condition=%wide.region_13.14_spmd, body=%wide.region_12.13_spmd.sunk | while | flops 524290 | bytes 6291517 | solution.py:176
  80.0 2.1 %add.203 = f32[1024,512]{1,0:T(8,128)S(1)} add(f32[1024,512]{1,0:T(8,128)S(1)} %get-tuple-element.819, f32[1024,512]{1,0:T(8,128)} %get-tuple-element.826) | non-fusion elementwise | flops 524288 | bytes 6291456 | tf_op jit(solution)/shard_map/while/body/add | solution.py:172
  82.2 0.1 convert_element_type.43
  82.3 0.1 pad_maximum_fusion
  82.5 1.2 %reshape_reshape.3 = bf16[32,8,4,640]{3,2,1,0:T(4,128)(2,1)} reshape(bf16[1024,640]{1,0:T(8,128)(2,1)S(1)} %pad_maximum_fusion) | data formatting | bytes 2621440 | tf_op jit(solution)/shard_map/reshape;reshape | solution.py:40
  83.7 1.8 %copy.27 = bf16[8,32,4,640]{3,2,1,0:T(4,128)(2,1)S(1)} copy(bf16[8,32,4,640]{3,2,0,1:T(4,128)(2,1)} %bitcast.20) | data formatting | bytes 2621440 | tf_op jit(solution)/shard_map/transpose | solution.py:41
  85.5 22.8 %all_to_all.34 = bf16[8,32,4,640]{3,2,1,0:T(4,128)(2,1)S(1)} all-to-all(bf16[8,32,4,640]{3,2,1,0:T(4,128)(2,1)S(1)} %copy.27), channel_id=1, replica_groups=mesh['dp_0'=8,'dp_1'=4,'dp_2'=4,'rep'=2] {'dp_2','rep'}, dimensions={0} | all-to-all | bytes 2621440 | tf_op jit(solution)/shard_map/all_to_all | solution.py:46
  108.2 0.7 reduce_sum.107
  108.9 13.2 %all_to_all.35 = bf16[32,4,640]{2,1,0:T(4,128)(2,1)S(1)} all-to-all(bf16[32,4,640]{2,1,0:T(4,128)(2,1)S(1)} %reduce_sum.107), channel_id=1, replica_groups=mesh['dp_0'=8,'dp_1'=4,'dp_2'=4,'rep'=2] {'dp_0','dp_1'}, dimensions={0} | all-to-all | bytes 327680 | tf_op jit(solution)/shard_map/all_to_all | solution.py:54
  122.2 0.6 split.9
  122.8 0.6 split.8
  (29 shorter events, 0.2 us)
Async XLA Ops:
  0.6 1.5 %copy-start = (bf16[512,1024]{1,0:T(8,128)(2,1)S(1)}, bf16[512,1024]{1,0:T(8,128)(2,1)}, u32[]{:S(2)}) copy-start(bf16[512,1024]{1,0:T(8,128)(2,1)} %param.20) | copy-start | bytes 3145732
  4.7 36.5 %copy-start.4 = (f32[1024]{0:T(1024)S(1)}, f32[1024]{0:T(1024)}, u32[]{:S(2)}) copy-start(f32[1024]{0:T(1024)} %param.21) | copy-start | bytes 12292
  5.7 37.9 %copy-start.1 = (f32[256,1024]{1,0:T(8,128)S(1)}, f32[256,1024]{1,0:T(8,128)}, u32[]{:S(2)}) copy-start(f32[256,1024]{1,0:T(8,128)} %get-tuple-element.760) | copy-start | bytes 3145732
  5.7 37.9 %copy-start.2 = (bf16[1024,128]{1,0:T(8,128)(2,1)S(1)}, bf16[1024,128]{1,0:T(8,128)(2,1)}, u32[]{:S(2)}) copy-start(bf16[1024,128]{1,0:T(8,128)(2,1)} %param.23) | copy-start | bytes 786436
  5.7 37.9 %copy-start.3 = (bf16[256,128]{1,0:T(8,128)(2,1)S(1)}, bf16[256,128]{1,0:T(8,128)(2,1)}, u32[]{:S(2)}) copy-start(bf16[256,128]{1,0:T(8,128)(2,1)} %param.25) | copy-start | bytes 196612
  5.7 37.9 %copy-start.5 = (f32[1024]{0:T(1024)S(1)}, f32[1024]{0:T(1024)}, u32[]{:S(2)}) copy-start(f32[1024]{0:T(1024)} %param.22) | copy-start | bytes 12292
  5.7 37.9 %copy-start.6 = (f32[128]{0:T(128)S(1)}, f32[128]{0:T(128)}, u32[]{:S(2)}) copy-start(f32[128]{0:T(128)} %param.24) | copy-start | bytes 1540
  17.5 22.5 %all-to-all-start.1 = ((f32[32,1,2049]{2,1,0:T(1,128)}), f32[32,1,2049]{2,1,0:T(1,128)S(1)}, u32[]{:S(2)}, u32[]{:S(2)}) async-start(f32[32,1,2049]{2,1,0:T(1,128)} %broadcast_in_dim.89), calls=%async_computation.1 | async-start | bytes 557056 | tf_op jit(solution)/shard_map/all_to_all | solution.py:17
  48.6 27.1 %copy-start.8 = (s32[512]{0:T(512)S(1)}, s32[512]{0:T(512)}, u32[]{:S(2)}) copy-start(s32[512]{0:T(512)} %param.19) | copy-start | bytes 6148
  48.6 27.1 %copy-start.9 = (s32[512]{0:T(512)S(1)}, s32[512]{0:T(512)}, u32[]{:S(2)}) copy-start(s32[512]{0:T(512)} %param.18) | copy-start | bytes 6148
  59.3 15.1 %all-to-all-start.3 = ((f32[32,1,2048]{2,1,0:T(1,128)}), f32[32,1,2048]{2,1,0:T(1,128)S(1)}, u32[]{:S(2)}, u32[]{:S(2)}) async-start(f32[32,1,2048]{2,1,0:T(1,128)} %broadcast_in_dim.92), calls=%async_computation.3 | async-start | bytes 524288 | tf_op jit(solution)/shard_map/all_to_all | solution.py:17
  75.7 4.1 %copy-start.7 = (f32[1024]{0:T(1024)}, f32[1024]{0:T(1024)S(1)}, u32[]{:S(2)}) copy-start(f32[1024]{0:T(1024)S(1)} %get-tuple-element.546) | copy-start | bytes 12292
where the time goes:
time: 124 us; the launch traced here: 123 us
  blocking collectives  56.5 us (46%)
  waiting for transfers between devices  22.6 us (18%)
  starting transfers between devices  14.9 us (12%)
  local copies, waits for them, and re-layouts  10.6 us (9%)
  matrix products  9.03 us (7%)
  other arithmetic  7.46 us (6%)
  between operations  2.19 us (2%)
    all_to_all x1, blocking collectives, sent_and_summed(): lax.all_to_all(pieces, axis, split_axis=0, concat_axis=0, tiled=True)  22.8 us
    all_to_all x2, waiting for transfers between devices, sent_to_all(): return lax.all_to_all(copies, axis, split_axis=0, concat_axis=0, tiled=True)  22.6 us
    all_to_all x2, blocking collectives, sent_to_all(): return lax.all_to_all(copies, axis, split_axis=0, concat_axis=0, tiled=True)  20.5 us
    all_to_all x2, starting transfers between devices, sent_to_all(): return lax.all_to_all(copies, axis, split_axis=0, concat_axis=0, tiled=True)  14.9 us
    all_to_all x1, blocking collectives, summed_rows(): lax.all_to_all(nearer.astype(jnp.bfloat16), far, split_axis=0, concat_axi...  13.2 us
    dot_general x1, matrix products, third_pass(): lax.dot_general(signal_block(), code_rows, (((0,), (0,)), ((), ())), pref...  4.04 us
  transfers between devices with their start and end apart: 2, of which 2 were waited for; matrix products, arithmetic and copies ran while one was open for 0% of the time, Pallas kernels for 0%

commit v1 on v0

v1 whole, which is shorter than its diff:
```python
import functools

import jax
import jax.numpy as jnp
from jax import lax
from jax.experimental import pallas as pl
from jax.experimental.pallas import tpu as pltpu
from jax.sharding import Mesh
from jax.sharding import PartitionSpec as P

AXES = ("z", "x", "y", "c")
MESH = pl.DeviceIdType.MESH
F32 = jnp.float32
BF16 = jnp.bfloat16
MODULUS = 65521
EPSILON = 1e-05
TOTAL = 16384.0
ROWS = 256
CODES = 512
GROUP = 8
PEERS = 32

NN = (((1,), (0,)), ((), ()))
NT = (((1,), (1,)), ((), ()))
TN = (((0,), (0,)), ((), ()))


def dot(a, b, dims=NN):
    return lax.dot_general(a, b, dims, preferred_element_type=F32)


def exact_pick(values, onehot):
    high = values.astype(BF16)
    rest = values - high.astype(F32)
    mid = rest.astype(BF16)
    low = (rest - mid.astype(F32)).astype(BF16)
    return dot(high, onehot) + dot(mid, onehot) + dot(low, onehot)


def iota(shape, dim):
    return lax.broadcasted_iota(jnp.int32, shape, dim)


def hidden_pick(q):
    i = iota((128, 1024), 0)
    h = iota((128, 1024), 1)
    return jnp.where(h == (i // 4) * 32 + q * 4 + i % 4, 1.0, 0.0).astype(BF16)


def lane_pick(q):
    lane = iota((128, 128), 0)
    i = iota((128, 128), 1)
    return jnp.where(lane == ((i % 16) // 4) * 32 + q * 4 + i % 4, 1.0, 0.0).astype(BF16)


def lane_put(q):
    i = iota((128, 128), 0)
    lane = iota((128, 128), 1)
    return jnp.where(lane == ((i % 16) // 4) * 32 + q * 4 + i % 4, 1.0, 0.0).astype(BF16)


def mish_terms(val):
    u = jnp.exp(jnp.minimum(val, 20.0))
    n = u * (u + 2.0)
    r = 1.0 / (n + 2.0)
    return u, n, r


def kernel(
    ids_ref, count_ref, scale_ref, shift_ref, wcode_ref, gain_ref, bias_ref, wout_ref, obias_ref, cot_ref,
    emb_ref, gcode_ref, gout_ref, ggain_ref, gbias_ref,
    idf, delta, code, pre, gact, dval, act, wown, wout_own, vec,
    st, st2, par, tot, p_send, p_recv, a_send, a_recv,
    s_id, r_id, s_dl, r_dl, s_st, r_st, s_p, r_p, s_par, r_par, s_st2, r_st2, s_a, r_a, s_tot, r_tot,
):
    z, x, y, c = (lax.axis_index(a) for a in AXES)
    q = y * 2 + c
    zx = z * 4 + x

    def far(k):
        t = lax.rem(zx + k, PEERS)
        return (t // 4, lax.rem(t, 4), y, c), t

    def near(k):
        t = lax.rem(q + k, GROUP)
        return (z, x, t // 2, lax.rem(t, 2)), t

    barrier = pltpu.get_barrier_semaphore()

    def greet_far(k, _):
        pl.semaphore_signal(barrier, inc=1, device_id=far(k)[0], device_id_type=MESH)
        return 0

    def greet_near(k, _):
        pl.semaphore_signal(barrier, inc=1, device_id=near(k)[0], device_id_type=MESH)
        return 0

    lax.fori_loop(1, GROUP, greet_near, 0)
    lax.fori_loop(1, PEERS, greet_far, 0)

    def to_near(buf, send, recv):
        def go(k, _):
            pltpu.make_async_remote_copy(
                buf.at[q], buf.at[q], send, recv, device_id=near(k)[0], device_id_type=MESH
            ).start()
            return 0

        lax.fori_loop(1, GROUP, go, 0)

    def to_far(buf, send, recv):
        def go(k, _):
            pltpu.make_async_remote_copy(
                buf.at[zx], buf.at[zx], send, recv, device_id=far(k)[0], device_id_type=MESH
            ).start()
            return 0

        lax.fori_loop(1, PEERS, go, 0)

    def scatter_far(src, dst, send, recv):
        def go(k, _):
            where, t = far(k)
            pltpu.make_async_remote_copy(
                src.at[t // 2, lax.rem(t, 2)], dst.at[zx], send, recv, device_id=where, device_id_type=MESH
            ).start()
            return 0

        lax.fori_loop(1, PEERS, go, 0)

    def wait(buf, n, sem):
        part = buf.at[pl.ds(0, n)]
        pltpu.make_async_copy(part, part, sem).wait()

    count = count_ref[0]
    slot = iota((2, 128), 0) * 128 + iota((2, 128), 1)
    idf[q] = jnp.where(slot < count, ids_ref[...].astype(F32), -1.0)
    live = iota((ROWS, 128), 0) < count
    delta[q] = jnp.where(live, cot_ref[...].astype(F32) * (1.0 / 128.0), 0.0).astype(BF16)

    pick = hidden_pick(q)
    wown[...] = dot(wcode_ref[...], pick, NT).astype(BF16)
    wout_own[...] = dot(pick, wout_ref[...]).astype(BF16)
    small = lane_pick(q)
    own_z = iota((8, 128), 0) == iota((8, 128), 1) // 16
    vec[0:1] = jnp.sum(jnp.where(own_z, exact_pick(gain_ref[...], small), 0.0), axis=0, keepdims=True)
    vec[1:2] = jnp.sum(jnp.where(own_z, exact_pick(bias_ref[...], small), 0.0), axis=0, keepdims=True)

    pl.semaphore_wait(barrier, PEERS - 1 + GROUP - 1)
    to_near(idf, s_id, r_id)
    to_near(delta, s_dl, r_dl)

    eye = iota((128, 128), 0) == iota((128, 128), 1)

    def hash_rows(qq, carry):
        total, square = carry
        for half in range(2):
            row = idf[qq, half : half + 1, :]
            ident = jnp.sum(jnp.where(eye, row, 0.0), axis=1, keepdims=True)
            alive = ident >= 0.0
            resid = ident.astype(jnp.int32)
            mixed = scale_ref[...] * resid + shift_ref[...]
            folded = (mixed & 65535) + 15 * lax.shift_right_logical(mixed, 16)
            value = folded.astype(F32)
            times = jnp.floor((value + 0.5) * (1.0 / MODULUS))
            bucket = value - times * float(MODULUS)
            rows = jnp.where(alive, bucket * (2.0 / (MODULUS - 1)) - 1.0, 0.0).astype(BF16)
            at = pl.multiple_of(qq * ROWS + half * 128, 128)
            code[pl.ds(at, 128), :] = rows
            hidden = dot(rows, wown[...])
            pre[pl.ds(at, 128), :] = hidden
            total = total + jnp.sum(hidden, axis=0, keepdims=True)
            square = square + jnp.sum(hidden * hidden, axis=0, keepdims=True)
        return total, square

    zero = jnp.zeros((1, 128), F32)
    sums = hash_rows(q, (zero, zero))
    wait(idf, GROUP - 1, r_id)
    sums = lax.fori_loop(1, GROUP, lambda k, s: hash_rows(near(k)[1], s), sums)
    st[zx] = jnp.concatenate(sums, axis=0)
    to_far(st, s_st, r_st)

    def stacked(full, lo):
        tiles = full.reshape(16, 8, full.shape[1])
        part = tiles[:, lo : lo + 4, :]
        return jnp.concatenate([part[:, :, :256], part[:, :, 256:]], axis=1)

    p_full = dot(pre[...].astype(BF16), code[...], TN)
    for parity in range(2):
        p_send[:, parity] = stacked(p_full, parity * 4).astype(BF16)
    p_recv[zx] = p_send[zx // 2, lax.rem(zx, 2)]
    scatter_far(p_send, p_recv, s_p, r_p)
    code_sum = dot(jnp.ones((8, GROUP * ROWS), BF16), code[...])[0:1]

    wait(delta, GROUP - 1, r_dl)

    def back_rows(b, _):
        at = pl.multiple_of(b * ROWS, ROWS)
        gact[pl.ds(at, ROWS), :] = dot(delta[b], wout_own[...], NT)
        return 0

    lax.fori_loop(0, GROUP, back_rows, 0)

    wait(st, PEERS - 1, r_st)
    moments = jnp.sum(st[...], axis=0) * (1.0 / TOTAL)
    mean = moments[0:1]
    inv_std = lax.rsqrt(moments[1:2] - mean * mean + EPSILON)
    gain = vec[0:1]
    bias = vec[1:2]
    par[q] = jnp.concatenate([mean, inv_std * gain, bias, bias], axis=0)
    to_near(par, s_par, r_par)

    def second(b, carry):
        sum_gain, sum_bias = carry
        at = pl.multiple_of(b * ROWS, ROWS)
        normed = (pre[pl.ds(at, ROWS), :] - mean) * inv_std
        val = normed * gain + bias
        u, n, r = mish_terms(val)
        act[b] = (val * (n * r)).astype(BF16)
        slope = r * (n + 4.0 * val * (u * (1.0 + u)) * r)
        d = gact[pl.ds(at, ROWS), :] * slope
        dval[pl.ds(at, ROWS), :] = d.astype(BF16)
        return (
            sum_gain + jnp.sum(d * normed, axis=0, keepdims=True),
            sum_bias + jnp.sum(d, axis=0, keepdims=True),
        )

    sums = lax.fori_loop(0, GROUP, second, (zero, zero))
    st2[zx] = jnp.concatenate(sums, axis=0)
    to_far(st2, s_st2, r_st2)

    a_full = dot(dval[...], code[...], TN)
    o_full = dot(act[...].reshape(GROUP * ROWS, 128), delta[...].reshape(GROUP * ROWS, 128), TN)
    s_rows = jnp.concatenate([code_sum[:, 128 * i : 128 * i + 128] for i in range(4)], axis=0)
    s_tiles = jnp.broadcast_to(s_rows[None], (16, 4, 128))
    o_tiles = o_full.reshape(16, 8, 128)
    for parity in range(2):
        a_send[:, parity, :, 0:256] = stacked(a_full, parity * 4).astype(BF16)
        both = jnp.concatenate([o_tiles[:, parity * 4 : parity * 4 + 4, :], s_tiles], axis=1)
        a_send[:, parity, :, 256:384] = both.astype(BF16)
    a_recv[zx] = a_send[zx // 2, lax.rem(zx, 2)]
    scatter_far(a_send, a_recv, s_a, r_a)

    wait(par, GROUP - 1, r_par)
    own_at = pl.multiple_of(q * ROWS, ROWS)

    def embed(k, acc):
        unit = hidden_pick(k)
        weights = dot(wcode_ref[...], unit, NT).astype(BF16)
        outward = dot(unit, wout_ref[...]).astype(BF16)
        hidden = dot(code[pl.ds(own_at, ROWS), :], weights)
        p = par[k]
        val = (hidden - p[0:1]) * p[1:2] + p[2:3]
        _, n, r = mish_terms(val)
        return acc + dot((val * (n * r)).astype(BF16), outward)

    acc = lax.fori_loop(0, GROUP, embed, jnp.zeros((ROWS, 128), F32))
    live = iota((ROWS, 128), 0) < count
    emb_ref[...] = jnp.where(live, acc + obias_ref[...], 0.0).astype(BF16)

    wait(st2, PEERS - 1, r_st2)
    sums = jnp.sum(st2[...], axis=0)
    tot[q] = sums
    to_near(tot, s_tot, r_tot)

    k1 = inv_std * gain
    k3 = k1 * inv_std * sums[0:1] * (1.0 / TOTAL)
    k2 = k1 * sums[1:2] * (1.0 / TOTAL) - k3 * mean
    mine = iota((8, 128), 1) == zx * 4 + iota((8, 128), 0) % 4

    def column(v):
        return jnp.sum(jnp.where(mine, v, 0.0), axis=1, keepdims=True)

    wait(p_recv, PEERS - 1, r_p)
    p_sum = jnp.sum(p_recv[...].astype(F32), axis=0)
    wait(a_recv, PEERS - 1, r_a)
    a_sum = jnp.sum(a_recv[...].astype(F32), axis=0)
    s_all = a_sum[4:8, 256:384]
    upper = jnp.concatenate([s_all[0:1], s_all[1:2]], axis=1)
    lower = jnp.concatenate([s_all[2:3], s_all[3:4]], axis=1)
    s_both = jnp.where(iota((8, 256), 0) < 4, upper, lower)
    grad = column(k1) * a_sum[:, 0:256] - column(k2) * s_both - column(k3) * p_sum
    gcode_ref[...] = jnp.concatenate([grad[0:4], grad[4:8]], axis=1)
    gout_ref[...] = a_sum[0:4, 256:384]

    wait(tot, GROUP - 1, r_tot)
    in_gain = jnp.zeros((8, 128), F32)
    in_bias = jnp.zeros((8, 128), F32)
    for k in range(GROUP):
        put = lane_put(k)
        t = tot[k]
        in_gain = in_gain + exact_pick(jnp.where(own_z, t[0:1], 0.0), put)
        in_bias = in_bias + exact_pick(jnp.where(own_z, t[1:2], 0.0), put)
    ggain_ref[...] = in_gain
    gbias_ref[...] = in_bias

    wait(idf, GROUP - 1, s_id)
    wait(delta, GROUP - 1, s_dl)
    wait(st, PEERS - 1, s_st)
    wait(p_recv, PEERS - 1, s_p)
    wait(par, GROUP - 1, s_par)
    wait(st2, PEERS - 1, s_st2)
    wait(a_recv, PEERS - 1, s_a)
    wait(tot, GROUP - 1, s_tot)


def per_device(ids, counts, hash_scale, hash_shift, w_code, norm_gain, norm_bias, w_out, out_bias, cotangent):
    vmem = pl.BlockSpec(memory_space=pltpu.VMEM)
    smem = pl.BlockSpec(memory_space=pltpu.SMEM)
    dma = pltpu.SemaphoreType.DMA
    wide = GROUP * ROWS
    emb, gcode, gout, ggain, gbias = pl.pallas_call(
        kernel,
        out_shape=(
            jax.ShapeDtypeStruct((ROWS, 128), BF16),
            jax.ShapeDtypeStruct((4, CODES), F32),
            jax.ShapeDtypeStruct((4, 128), F32),
            jax.ShapeDtypeStruct((8, 128), F32),
            jax.ShapeDtypeStruct((8, 128), F32),
        ),
        in_specs=[vmem, smem] + [vmem] * 8,
        out_specs=(vmem,) * 5,
        scratch_shapes=[
            pltpu.VMEM((GROUP, 2, 128), F32),
            pltpu.VMEM((GROUP, ROWS, 128), BF16),
            pltpu.VMEM((wide, CODES), BF16),
            pltpu.VMEM((wide, 128), F32),
            pltpu.VMEM((wide, 128), F32),
            pltpu.VMEM((wide, 128), BF16),
            pltpu.VMEM((GROUP, ROWS, 128), BF16),
            pltpu.VMEM((CODES, 128), BF16),
            pltpu.VMEM((128, 128), BF16),
            pltpu.VMEM((8, 128), F32),
            pltpu.VMEM((PEERS, 2, 128), F32),
            pltpu.VMEM((PEERS, 2, 128), F32),
            pltpu.VMEM((GROUP, 4, 128), F32),
            pltpu.VMEM((GROUP, 2, 128), F32),
            pltpu.VMEM((16, 2, 8, 256), BF16),
            pltpu.VMEM((PEERS, 8, 256), BF16),
            pltpu.VMEM((16, 2, 8, 384), BF16),
            pltpu.VMEM((PEERS, 8, 384), BF16),
        ]
        + [dma] * 16,
        compiler_params=pltpu.CompilerParams(
            collective_id=0, has_side_effects=True, vmem_limit_bytes=48 << 20
        ),
    )(
        ids.reshape(2, 128),
        counts,
        hash_scale.reshape(1, CODES),
        hash_shift.reshape(1, CODES),
        w_code,
        norm_gain.reshape(8, 128),
        norm_bias.reshape(8, 128),
        w_out,
        out_bias.reshape(1, 128),
        cotangent,
    )
    return emb, gcode, gout, ggain.reshape(1024), gbias.reshape(1024)


def solution(mesh):
    finer = Mesh(mesh.devices.reshape(8, 4, 4, 2), AXES)
    return jax.shard_map(
        per_device,
        mesh=finer,
        in_specs=(P(AXES), P(AXES), P(), P(), P(), P(), P(), P(), P(), P(AXES, None)),
        out_specs=(P(AXES, None), P(AXES, None), P(AXES, None), P(), P()),
        check_vma=False,
    )
```

time: 124 us -> 48.9 us (0.39)
  blocking collectives: 56.5 us -> 0 us
  Pallas kernels: 0 us -> 39.9 us
  waiting for transfers between devices: 22.6 us -> 0 us
  starting transfers between devices: 14.9 us -> 0 us
  matrix products: 9.03 us -> 0 us
  other arithmetic: 7.46 us -> 0 us
  local copies, waits for them, and re-layouts: 10.6 us -> 7.35 us
    all_to_all x4 -> x0, blocking collectives: 56.5 us -> none  [the longest x1 22.8 us: sent_and_summed(): lax.all_to_all(pieces, axis, split_axis=0, concat_axis=0, tiled=True)]
    pallas_call x0 -> x1, Pallas kernels: none -> 39.9 us  [per_device(): pl.pallas_call(kernel, out_shape=(jax.ShapeDtypeStruct((ROWS, 128), BF16)...]
    all_to_all x2 -> x0, waiting for transfers between devices: 22.6 us -> none  [sent_to_all(): return lax.all_to_all(copies, axis, split_axis=0, concat_axis=0, tiled=True)]
    all_to_all x2 -> x0, starting transfers between devices: 14.9 us -> none  [sent_to_all(): return lax.all_to_all(copies, axis, split_axis=0, concat_axis=0, tiled=True)]
    dot_general x5 -> x0, matrix products: 9.03 us -> none  [the longest x1 4.04 us: third_pass(): lax.dot_general(signal_block(), code_rows, (((0,), (0,)), ((), ())), pref...]
    unnamed x20 -> x23, local copies, waits for them, and re-layouts: 0.05 us -> 7.35 us
    another operation x3 -> x0, local copies, waits for them, and re-layouts: 3.46 us -> none
    broadcast_in_dim x11 -> x0, local copies, waits for them, and re-layouts: 2.7 us -> none  [the longest x4 1.76 us: sent_to_all(): copies = jnp.broadcast_to(shard, (lax.axis_size(axis), *shard.shape))]
  transfers between devices with their start and end apart: 2 -> 0, of which waited for: 2 -> 0; matrix products, arithmetic and copies ran while one was open for 0% -> 0% of each run, Pallas kernels for 0% -> 0%
where the time goes in v1:
time: 48.9 us; the launch traced here: 48.6 us
  Pallas kernels  39.9 us (82%)
  local copies, waits for them, and re-layouts  7.35 us (15%)
  between operations  1.36 us (3%)
    pallas_call x1, Pallas kernels, per_device(): pl.pallas_call(kernel, out_shape=(jax.ShapeDtypeStruct((ROWS, 128), BF16)...  39.9 us
    unnamed x23, local copies, waits for them, and re-layouts  7.35 us

profile of v1, /device:TPU:1, one launch (start us, length us, event | category | flops | bytes accessed | tf_op | source)
XLA Modules:
  0.0 48.6 jit_solution(1144703933499602724)
XLA Ops:
  0.6 0.0 copy-start.6
  1.3 0.0 copy-start.5
  1.3 0.0 copy-start.4
  1.3 0.0 copy-start.3
  1.3 0.0 copy-start.7
  1.3 0.0 copy-done.6
  1.4 0.6 %copy-done.5 = s32[512]{0:T(512)S(1)} copy-done((s32[512]{0:T(512)S(1)}, s32[512]{0:T(512)}, u32[]{:S(2)}) %copy-start.5) | copy-done | bytes 2072
  2.0 0.0 copy-done.4
  2.0 0.0 copy-done.3
  2.0 0.0 copy-done.7
  2.0 0.0 copy-start
  2.0 1.2 %copy-done = bf16[512,1024]{1,0:T(8,128)(2,1)S(1)} copy-done((bf16[512,1024]{1,0:T(8,128)(2,1)S(1)}, bf16[512,1024]{1,0:T(8,128)(2,1)}, u32[]{:S(2)}) %copy-start) | copy-done | bytes 1048600
  3.3 0.0 copy-start.1
  3.3 0.9 %copy-done.1 = bf16[1024,128]{1,0:T(8,128)(2,1)S(1)} copy-done((bf16[1024,128]{1,0:T(8,128)(2,1)S(1)}, bf16[1024,128]{1,0:T(8,128)(2,1)}, u32[]{:S(2)}) %copy-start.1) | copy-done | bytes 262168
  4.2 0.0 copy-start.2
  4.2 0.8 %copy-done.2 = bf16[256,128]{1,0:T(8,128)(2,1)S(1)} copy-done((bf16[256,128]{1,0:T(8,128)(2,1)S(1)}, bf16[256,128]{1,0:T(8,128)(2,1)}, u32[]{:S(2)}) %copy-start.2) | copy-done | bytes 65560
  5.0 0.0 copy-start.8
  5.0 0.7 %copy-done.8 = f32[128]{0:T(128)S(1)} copy-done((f32[128]{0:T(128)S(1)}, f32[128]{0:T(128)}, u32[]{:S(2)}) %copy-start.8) | copy-done | bytes 536
  5.7 39.9 %shard_map.137 = (bf16[256,128]{1,0:T(8,128)(2,1)S(1)}, f32[4,512]{1,0:T(4,128)S(1)}, f32[4,128]{1,0:T(4,128)S(1)}, f32[8,128]{1,0:T(8,128)S(1)}, f32[8,128]{1,0:T(8,128)S(1)}) custom-call(s32[2,128]{1,0:T(2,128)S(1)} %bitcast.14, s32[1]{0:T(128)S(6)} %copy.20.count_ref, s32[1,512]{1,0:T(1,128)S(1)} %bitcast.12, s32[1,512]{1,0:T(1,128)S(1)} %bitcast.13, ...), custom_call_target="tpu_custom_call" | custom-call | tf_op jit(solution)/shard_map/pallas_call | solution.py:310
  45.6 0.6 %copy.21 = bf16[256,128]{1,0:T(8,128)(2,1)} copy(bf16[256,128]{1,0:T(8,128)(2,1)S(1)} %get-tuple-element.20) | data formatting | bytes 131072
  46.3 0.6 %copy.22 = f32[4,512]{1,0:T(4,128)} copy(f32[4,512]{1,0:T(4,128)S(1)} %get-tuple-element.21) | data formatting | bytes 16384
  46.9 0.6 %copy.23 = f32[4,128]{1,0:T(4,128)} copy(f32[4,128]{1,0:T(4,128)S(1)} %get-tuple-element.22) | data formatting | bytes 4096
  47.4 0.6 %copy.24 = f32[1024]{0:T(1024)} copy(f32[1024]{0:T(1024)S(1)} %bitcast.11) | data formatting | bytes 8192
  48.0 0.6 %copy.25 = f32[1024]{0:T(1024)} copy(f32[1024]{0:T(1024)S(1)} %bitcast.10) | data formatting | bytes 8192
Async XLA Ops:
  0.6 0.7 %copy-start.6 = (s32[512]{0:T(512)S(1)}, s32[512]{0:T(512)}, u32[]{:S(2)}) copy-start(s32[512]{0:T(512)} %param.13) | copy-start | bytes 6148
  1.3 0.7 %copy-start.5 = (s32[512]{0:T(512)S(1)}, s32[512]{0:T(512)}, u32[]{:S(2)}) copy-start(s32[512]{0:T(512)} %param.12) | copy-start | bytes 6148
  1.3 0.7 %copy-start.4 = (f32[1024]{0:T(1024)S(1)}, f32[1024]{0:T(1024)}, u32[]{:S(2)}) copy-start(f32[1024]{0:T(1024)} %param.16) | copy-start | bytes 12292
  1.3 0.7 %copy-start.3 = (f32[1024]{0:T(1024)S(1)}, f32[1024]{0:T(1024)}, u32[]{:S(2)}) copy-start(f32[1024]{0:T(1024)} %param.15) | copy-start | bytes 12292
  1.3 0.7 %copy-start.7 = (s32[256]{0:T(256)S(1)}, s32[256]{0:T(256)}, u32[]{:S(2)}) copy-start(s32[256]{0:T(256)} %param.10) | copy-start | bytes 3076
  2.0 1.2 %copy-start = (bf16[512,1024]{1,0:T(8,128)(2,1)S(1)}, bf16[512,1024]{1,0:T(8,128)(2,1)}, u32[]{:S(2)}) copy-start(bf16[512,1024]{1,0:T(8,128)(2,1)} %wcode_ref.1) | copy-start | bytes 3145732
  3.3 0.9 %copy-start.1 = (bf16[1024,128]{1,0:T(8,128)(2,1)S(1)}, bf16[1024,128]{1,0:T(8,128)(2,1)}, u32[]{:S(2)}) copy-start(bf16[1024,128]{1,0:T(8,128)(2,1)} %wout_ref.1) | copy-start | bytes 786436
  4.2 0.8 %copy-start.2 = (bf16[256,128]{1,0:T(8,128)(2,1)S(1)}, bf16[256,128]{1,0:T(8,128)(2,1)}, u32[]{:S(2)}) copy-start(bf16[256,128]{1,0:T(8,128)(2,1)} %cot_ref.1) | copy-start | bytes 196612
  5.0 0.7 %copy-start.8 = (f32[128]{0:T(128)S(1)}, f32[128]{0:T(128)}, u32[]{:S(2)}) copy-start(f32[128]{0:T(128)} %param.18) | copy-start | bytes 1540

commit v2 on v1

--- a/solution.py
+++ b/solution.py
@@ -14,6 +14,7 @@
 BF16 = jnp.bfloat16
 MODULUS = 65521
 EPSILON = 1e-05
+MAGIC = 12582912.0
 TOTAL = 16384.0
 ROWS = 256
 CODES = 512
@@ -29,16 +30,21 @@
     return lax.dot_general(a, b, dims, preferred_element_type=F32)
 
 
-def exact_pick(values, onehot):
+def iota(shape, dim):
+    return lax.broadcasted_iota(jnp.int32, shape, dim)
+
+
+def parts(values):
     high = values.astype(BF16)
     rest = values - high.astype(F32)
     mid = rest.astype(BF16)
     low = (rest - mid.astype(F32)).astype(BF16)
+    return high, mid, low
+
+
+def exact_pick(values, onehot):
+    high, mid, low = parts(values)
     return dot(high, onehot) + dot(mid, onehot) + dot(low, onehot)
-
-
-def iota(shape, dim):
-    return lax.broadcasted_iota(jnp.int32, shape, dim)
 
 
 def hidden_pick(q):
@@ -67,9 +73,10 @@
 
 
 def kernel(
-    ids_ref, count_ref, scale_ref, shift_ref, wcode_ref, gain_ref, bias_ref, wout_ref, obias_ref, cot_ref,
+    count_ref, ids_hbm, scale_hbm, shift_hbm, gain_hbm, bias_hbm, wcode_hbm, wout_hbm, cot_hbm, obias_hbm,
     emb_ref, gcode_ref, gout_ref, ggain_ref, gbias_ref,
-    idf, delta, code, pre, gact, dval, act, wown, wout_own, vec,
+    ids_ref, scale_ref, shift_ref, gain_ref, bias_ref, wcode_ref, wout_ref, cot_ref, obias_ref, s_in,
+    idf, delta, code, pre, gact, dval, act, wown, wout_own, vec, put, mix, nat,
     st, st2, par, tot, p_send, p_recv, a_send, a_recv,
     s_id, r_id, s_dl, r_dl, s_st, r_st, s_p, r_p, s_par, r_par, s_st2, r_st2, s_a, r_a, s_tot, r_tot,
 ):
@@ -77,13 +84,38 @@
     q = y * 2 + c
     zx = z * 4 + x
 
+    def fold(m):
+        return (m // 2 + m % 2) * (1 - 2 * (m % 2))
+
     def far(k):
-        t = lax.rem(zx + k, PEERS)
-        return (t // 4, lax.rem(t, 4), y, c), t
+        tz = lax.rem(z + 4 + fold(k // 4) + 8, 8)
+        tx = lax.rem(x + 2 + fold(k % 4) + 4, 4)
+        return (tz, tx, y, c), tz * 4 + tx
 
     def near(k):
-        t = lax.rem(q + k, GROUP)
-        return (z, x, t // 2, lax.rem(t, 2)), t
+        m = k // 2
+        ty = lax.rem(y + m + (m // 2) * (5 - 2 * m), 4)
+        tc = lax.rem(c + k % 2, 2)
+        return (z, x, ty, tc), ty * 2 + tc
+
+    loads = [
+        pltpu.make_async_copy(src, dst, s_in.at[i])
+        for i, (src, dst) in enumerate(
+            (
+                (ids_hbm, ids_ref),
+                (cot_hbm, cot_ref),
+                (wcode_hbm, wcode_ref),
+                (wout_hbm, wout_ref),
+                (scale_hbm, scale_ref),
+                (shift_hbm, shift_ref),
+                (gain_hbm, gain_ref),
+                (bias_hbm, bias_ref),
+                (obias_hbm, obias_ref),
+            )
+        )
+    ]
+    for load in loads:
+        load.start()
 
     barrier = pltpu.get_barrier_semaphore()
 
@@ -95,8 +127,8 @@
         pl.semaphore_signal(barrier, inc=1, device_id=near(k)[0], device_id_type=MESH)
         return 0
 
+    lax.fori_loop(0, PEERS - 1, greet_far, 0)
     lax.fori_loop(1, GROUP, greet_near, 0)
-    lax.fori_loop(1, PEERS, greet_far, 0)
 
     def to_near(buf, send, recv):
         def go(k, _):
@@ -114,7 +146,7 @@
             ).start()
             return 0
 
-        lax.fori_loop(1, PEERS, go, 0)
+        lax.fori_loop(0, PEERS - 1, go, 0)
 
     def scatter_far(src, dst, send, recv):
         def go(k, _):
@@ -124,57 +156,71 @@
             ).start()
             return 0
 
-        lax.fori_loop(1, PEERS, go, 0)
+        lax.fori_loop(0, PEERS - 1, go, 0)
 
     def wait(buf, n, sem):
         part = buf.at[pl.ds(0, n)]
         pltpu.make_async_copy(part, part, sem).wait()
 
     count = count_ref[0]
+    loads[0].wait()
     slot = iota((2, 128), 0) * 128 + iota((2, 128), 1)
     idf[q] = jnp.where(slot < count, ids_ref[...].astype(F32), -1.0)
+    pl.semaphore_wait(barrier, PEERS - 1 + GROUP - 1)
+    to_near(idf, s_id, r_id.at[q])
+
+    loads[1].wait()
     live = iota((ROWS, 128), 0) < count
     delta[q] = jnp.where(live, cot_ref[...].astype(F32) * (1.0 / 128.0), 0.0).astype(BF16)
-
+    to_near(delta, s_dl, r_dl)
+
+    for load in loads[2:]:
+        load.wait()
     pick = hidden_pick(q)
     wown[...] = dot(wcode_ref[...], pick, NT).astype(BF16)
+
+    scale = scale_ref[...].astype(F32)
+    high = scale * 256.0
+    mix[0:1] = high - ((high * (1.0 / MODULUS) + MAGIC) - MAGIC) * float(MODULUS)
+    mix[1:2] = scale
+    mix[2:3] = shift_ref[...].astype(F32)
+
+    eye = iota((128, 128), 0) == iota((128, 128), 1)
+
+    def hash_rows(qq, carry):
+        total, square = carry
+        pair = idf[qq]
+        ident = jnp.concatenate(
+            [jnp.sum(jnp.where(eye, pair[h : h + 1], 0.0), axis=1, keepdims=True) for h in range(2)], axis=0
+        )
+        upper = jnp.floor(ident * (1.0 / 256.0))
+        lower = ident - upper * 256.0
+        value = mix[0:1] * upper + (mix[1:2] * lower + mix[2:3])
+        times = (value * (1.0 / MODULUS) + MAGIC) - MAGIC
+        bucket = value - times * float(MODULUS)
+        bucket = jnp.where(bucket < 0.0, bucket + float(MODULUS), bucket)
+        rows = (bucket * (2.0 / (MODULUS - 1)) - 1.0).astype(BF16)
+        at = pl.multiple_of(qq * ROWS, ROWS)
+        code[pl.ds(at, ROWS), :] = rows
+        hidden = jnp.where(ident >= 0.0, dot(rows, wown[...]), 0.0)
+        pre[pl.ds(at, ROWS), :] = hidden
+        total = total + jnp.sum(hidden, axis=0, keepdims=True)
+        square = square + jnp.sum(hidden * hidden, axis=0, keepdims=True)
+        return total, square
+
+    def hash_next(k, sums):
+        other = near(k)[1]
+        pltpu.make_async_copy(idf.at[other], idf.at[other], r_id.at[other]).wait()
+        return hash_rows(other, sums)
+
+    zero = jnp.zeros((1, 128), F32)
+    sums = hash_rows(q, (zero, zero))
     wout_own[...] = dot(pick, wout_ref[...]).astype(BF16)
     small = lane_pick(q)
     own_z = iota((8, 128), 0) == iota((8, 128), 1) // 16
     vec[0:1] = jnp.sum(jnp.where(own_z, exact_pick(gain_ref[...], small), 0.0), axis=0, keepdims=True)
     vec[1:2] = jnp.sum(jnp.where(own_z, exact_pick(bias_ref[...], small), 0.0), axis=0, keepdims=True)
-
-    pl.semaphore_wait(barrier, PEERS - 1 + GROUP - 1)
-    to_near(idf, s_id, r_id)
-    to_near(delta, s_dl, r_dl)
-
-    eye = iota((128, 128), 0) == iota((128, 128), 1)
-
-    def hash_rows(qq, carry):
-        total, square = carry
-        for half in range(2):
-            row = idf[qq, half : half + 1, :]
-            ident = jnp.sum(jnp.where(eye, row, 0.0), axis=1, keepdims=True)
-            alive = ident >= 0.0
-            resid = ident.astype(jnp.int32)
-            mixed = scale_ref[...] * resid + shift_ref[...]
-            folded = (mixed & 65535) + 15 * lax.shift_right_logical(mixed, 16)
-            value = folded.astype(F32)
-            times = jnp.floor((value + 0.5) * (1.0 / MODULUS))
-            bucket = value - times * float(MODULUS)
-            rows = jnp.where(alive, bucket * (2.0 / (MODULUS - 1)) - 1.0, 0.0).astype(BF16)
-            at = pl.multiple_of(qq * ROWS + half * 128, 128)
-            code[pl.ds(at, 128), :] = rows
-            hidden = dot(rows, wown[...])
-            pre[pl.ds(at, 128), :] = hidden
-            total = total + jnp.sum(hidden, axis=0, keepdims=True)
-            square = square + jnp.sum(hidden * hidden, axis=0, keepdims=True)
-        return total, square
-
-    zero = jnp.zeros((1, 128), F32)
-    sums = hash_rows(q, (zero, zero))
-    wait(idf, GROUP - 1, r_id)
-    sums = lax.fori_loop(1, GROUP, lambda k, s: hash_rows(near(k)[1], s), sums)
+    sums = lax.fori_loop(1, GROUP, hash_next, sums)
     st[zx] = jnp.concatenate(sums, axis=0)
     to_far(st, s_st, r_st)
 
@@ -188,7 +234,10 @@
         p_send[:, parity] = stacked(p_full, parity * 4).astype(BF16)
     p_recv[zx] = p_send[zx // 2, lax.rem(zx, 2)]
     scatter_far(p_send, p_recv, s_p, r_p)
-    code_sum = dot(jnp.ones((8, GROUP * ROWS), BF16), code[...])[0:1]
+    alive = jnp.concatenate([jnp.where(idf[b, h : h + 1, :] >= 0.0, 1.0, 0.0) for b in range(8) for h in range(2)], axis=1)
+    code_sum = dot(jnp.broadcast_to(alive, (8, GROUP * ROWS)).astype(BF16), code[...])[0:1]
+    for b in range(GROUP):
+        put[b * 128 : b * 128 + 128, :] = lane_put(b)
 
     wait(delta, GROUP - 1, r_dl)
 
@@ -198,6 +247,13 @@
         return 0
 
     lax.fori_loop(0, GROUP, back_rows, 0)
+
+    def in_order(ref):
+        blocks = [
+            jnp.concatenate([jnp.where(own_z, ref[b, v : v + 1, :], 0.0) for b in range(GROUP)], axis=1) for v in range(2)
+        ]
+        out = dot(jnp.concatenate(parts(jnp.concatenate(blocks, axis=0)), axis=0), put[...])
+        return out[0:16] + out[16:32] + out[32:48]
 
     wait(st, PEERS - 1, r_st)
     moments = jnp.sum(st[...], axis=0) * (1.0 / TOTAL)
@@ -205,7 +261,7 @@
     inv_std = lax.rsqrt(moments[1:2] - mean * mean + EPSILON)
     gain = vec[0:1]
     bias = vec[1:2]
-    par[q] = jnp.concatenate([mean, inv_std * gain, bias, bias], axis=0)
+    par[q] = jnp.concatenate([mean, inv_std], axis=0)
     to_near(par, s_par, r_par)
 
     def second(b, carry):
@@ -240,17 +296,17 @@
     scatter_far(a_send, a_recv, s_a, r_a)
 
     wait(par, GROUP - 1, r_par)
+    ordered = in_order(par)
+    nat[0] = ordered[0:8]
+    nat[1] = ordered[8:16] * gain_ref[...]
     own_at = pl.multiple_of(q * ROWS, ROWS)
 
     def embed(k, acc):
-        unit = hidden_pick(k)
-        weights = dot(wcode_ref[...], unit, NT).astype(BF16)
-        outward = dot(unit, wout_ref[...]).astype(BF16)
-        hidden = dot(code[pl.ds(own_at, ROWS), :], weights)
-        p = par[k]
-        val = (hidden - p[0:1]) * p[1:2] + p[2:3]
+        at = pl.multiple_of(k * 128, 128)
+        hidden = dot(code[pl.ds(own_at, ROWS), :], wcode_ref[:, pl.ds(at, 128)])
+        val = (hidden - nat[0, pl.ds(k, 1), :]) * nat[1, pl.ds(k, 1), :] + bias_ref[pl.ds(k, 1), :]
         _, n, r = mish_terms(val)
-        return acc + dot((val * (n * r)).astype(BF16), outward)
+        return acc + dot((val * (n * r)).astype(BF16), wout_ref[pl.ds(at, 128), :])
 
     acc = lax.fori_loop(0, GROUP, embed, jnp.zeros((ROWS, 128), F32))
     live = iota((ROWS, 128), 0) < count
@@ -282,15 +338,9 @@
     gout_ref[...] = a_sum[0:4, 256:384]
 
     wait(tot, GROUP - 1, r_tot)
-    in_gain = jnp.zeros((8, 128), F32)
-    in_bias = jnp.zeros((8, 128), F32)
-    for k in range(GROUP):
-        put = lane_put(k)
-        t = tot[k]
-        in_gain = in_gain + exact_pick(jnp.where(own_z, t[0:1], 0.0), put)
-        in_bias = in_bias + exact_pick(jnp.where(own_z, t[1:2], 0.0), put)
-    ggain_ref[...] = in_gain
-    gbias_ref[...] = in_bias
+    ordered = in_order(tot)
+    ggain_ref[...] = ordered[0:8]
+    gbias_ref[...] = ordered[8:16]
 
     wait(idf, GROUP - 1, s_id)
     wait(delta, GROUP - 1, s_dl)
@@ -302,23 +352,43 @@
     wait(tot, GROUP - 1, s_tot)
 
 
+def store_kernel(*refs):
+    srcs, dsts, sem = refs[:5], refs[5:10], refs[10]
+    copies = [pltpu.make_async_copy(a, b, sem.at[i]) for i, (a, b) in enumerate(zip(srcs, dsts))]
+    for copy in copies:
+        copy.start()
+    for copy in copies:
+        copy.wait()
+
+
 def per_device(ids, counts, hash_scale, hash_shift, w_code, norm_gain, norm_bias, w_out, out_bias, cotangent):
     vmem = pl.BlockSpec(memory_space=pltpu.VMEM)
-    smem = pl.BlockSpec(memory_space=pltpu.SMEM)
+    hbm = pl.BlockSpec(memory_space=pltpu.HBM)
     dma = pltpu.SemaphoreType.DMA
     wide = GROUP * ROWS
-    emb, gcode, gout, ggain, gbias = pl.pallas_call(
+    shapes = (
+        jax.ShapeDtypeStruct((ROWS, 128), BF16),
+        jax.ShapeDtypeStruct((4, CODES), F32),
+        jax.ShapeDtypeStruct((4, 128), F32),
+        jax.ShapeDtypeStruct((8, 128), F32),
+        jax.ShapeDtypeStruct((8, 128), F32),
+    )
+    results = pl.pallas_call(
         kernel,
-        out_shape=(
-            jax.ShapeDtypeStruct((ROWS, 128), BF16),
-            jax.ShapeDtypeStruct((4, CODES), F32),
-            jax.ShapeDtypeStruct((4, 128), F32),
-            jax.ShapeDtypeStruct((8, 128), F32),
-            jax.ShapeDtypeStruct((8, 128), F32),
-        ),
-        in_specs=[vmem, smem] + [vmem] * 8,
+        out_shape=shapes,
+        in_specs=[pl.BlockSpec(memory_space=pltpu.SMEM)] + [hbm] * 9,
         out_specs=(vmem,) * 5,
         scratch_shapes=[
+            pltpu.VMEM((2, 128), jnp.int32),
+            pltpu.VMEM((1, CODES), jnp.int32),
+            pltpu.VMEM((1, CODES), jnp.int32),
+            pltpu.VMEM((8, 128), F32),
+            pltpu.VMEM((8, 128), F32),
+            pltpu.VMEM((CODES, 1024), BF16),
+            pltpu.VMEM((1024, 128), BF16),
+            pltpu.VMEM((ROWS, 128), BF16),
+            pltpu.VMEM((1, 128), F32),
+            dma((9,)),
             pltpu.VMEM((GROUP, 2, 128), F32),
             pltpu.VMEM((GROUP, ROWS, 128), BF16),
             pltpu.VMEM((wide, CODES), BF16),
@@ -329,31 +399,48 @@
             pltpu.VMEM((CODES, 128), BF16),
             pltpu.VMEM((128, 128), BF16),
             pltpu.VMEM((8, 128), F32),
+            pltpu.VMEM((1024, 128), BF16),
+            pltpu.VMEM((8, CODES), F32),
+            pltpu.VMEM((2, 8, 128), F32),
             pltpu.VMEM((PEERS, 2, 128), F32),
             pltpu.VMEM((PEERS, 2, 128), F32),
-            pltpu.VMEM((GROUP, 4, 128), F32),
+            pltpu.VMEM((GROUP, 2, 128), F32),
             pltpu.VMEM((GROUP, 2, 128), F32),
             pltpu.VMEM((16, 2, 8, 256), BF16),
             pltpu.VMEM((PEERS, 8, 256), BF16),
             pltpu.VMEM((16, 2, 8, 384), BF16),
             pltpu.VMEM((PEERS, 8, 384), BF16),
         ]
-        + [dma] * 16,
+        + [dma, dma((GROUP,))]
+        + [dma] * 14,
         compiler_params=pltpu.CompilerParams(
             collective_id=0, has_side_effects=True, vmem_limit_bytes=48 << 20
         ),
     )(
-        ids.reshape(2, 128),
         counts,
-        hash_scale.reshape(1, CODES),
-        hash_shift.reshape(1, CODES),
-        w_code,
-        norm_gain.reshape(8, 128),
-        norm_bias.reshape(8, 128),
-        w_out,
-        out_bias.reshape(1, 128),
-        cotangent,
+        *(
+            pltpu.with_memory_space_constraint(array, pltpu.HBM)
+            for array in (
+                ids.reshape(2, 128),
+                hash_scale.reshape(1, CODES),
+                hash_shift.reshape(1, CODES),
+                norm_gain.reshape(8, 128),
+                norm_bias.reshape(8, 128),
+                w_code,
+                w_out,
+                cotangent,
+                out_bias.reshape(1, 128),
+            )
+        ),
     )
+    emb, gcode, gout, ggain, gbias = pl.pallas_call(
+        store_kernel,
+        out_shape=shapes,
+        in_specs=[vmem] * 5,
+        out_specs=(hbm,) * 5,
+        scratch_shapes=[dma((5,))],
+        compiler_params=pltpu.CompilerParams(vmem_limit_bytes=4 << 20),
+    )(*results)
     return emb, gcode, gout, ggain.reshape(1024), gbias.reshape(1024)
 
 

time: 48.9 us -> 37.9 us (0.78)
  local copies, waits for them, and re-layouts: 7.35 us -> 0 us
  Pallas kernels: 39.9 us -> 36.5 us
    unnamed x23 -> x0, local copies, waits for them, and re-layouts: 7.35 us -> none
    pallas_call x1 -> x2, Pallas kernels: 39.9 us -> 36.5 us  [the longest x1 35.9 us: per_device(): pl.pallas_call(kernel, out_shape=shapes, in_specs=[pl.BlockSpec(memory_sp...]
where the time goes in v2:
time: 37.9 us; the launch traced here: 37.8 us
  Pallas kernels  36.5 us (96%)
  between operations  1.29 us (3%)
    pallas_call x1, Pallas kernels, per_device(): pl.pallas_call(kernel, out_shape=shapes, in_specs=[pl.BlockSpec(memory_sp...  35.9 us

profile of v2, /device:TPU:1, one launch (start us, length us, event | category | flops | bytes accessed | tf_op | source)
XLA Modules:
  0.0 37.8 jit_solution(12347731122424807206)
XLA Ops:
  1.3 35.9 %shard_map.137 = (bf16[256,128]{1,0:T(8,128)(2,1)S(1)}, f32[4,512]{1,0:T(4,128)S(1)}, f32[4,128]{1,0:T(4,128)S(1)}, f32[8,128]{1,0:T(8,128)S(1)}, f32[8,128]{1,0:T(8,128)S(1)}) custom-call(s32[1]{0:T(128)S(6)} %copy.15.count_ref, s32[2,128]{1,0:T(2,128)} %bitcast.12, s32[1,512]{1,0:T(1,128)} %bitcast.10, s32[1,512]{1,0:T(1,128)} %bitcast.11, ...), custom_call_target="tpu_custom_call" | custom-call | tf_op jit(solution)/shard_map/pallas_call | solution.py:376
  37.1 0.7 %shard_map.138 = (bf16[256,128]{1,0:T(8,128)(2,1)}, f32[4,512]{1,0:T(4,128)}, f32[4,128]{1,0:T(4,128)}, f32[8,128]{1,0:T(8,128)}, f32[8,128]{1,0:T(8,128)}) custom-call(bf16[256,128]{1,0:T(8,128)(2,1)S(1)} %get-tuple-element.15.refs_0_, f32[4,512]{1,0:T(4,128)S(1)} %get-tuple-element.16.refs_1_, f32[4,128]{1,0:T(4,128)S(1)} %get-tuple-element.17.refs_2_, ...), custom_call_target="tpu_custom_call" | custom-call | tf_op jit(solution)/shard_map/pallas_call | solution.py:436

commit v3 on v2

--- a/solution.py
+++ b/solution.py
@@ -20,6 +20,12 @@
 CODES = 512
 GROUP = 8
 PEERS = 32
+FAR = sorted(
+    ((dz, dx) for dz in range(8) for dx in range(4) if dz or dx),
+    key=lambda o: (-min(o[0], 8 - o[0]) - min(o[1], 4 - o[1]), o),
+)
+NEAR = [(0, 0), (0, 1), (1, 0), (3, 0), (1, 1), (3, 1), (2, 0), (2, 1)]
+BACK = [NEAR.index(((4 - dy) % 4, dc)) for dy, dc in NEAR]
 
 NN = (((1,), (0,)), ((), ()))
 NT = (((1,), (1,)), ((), ()))
@@ -53,10 +59,10 @@
     return jnp.where(h == (i // 4) * 32 + q * 4 + i % 4, 1.0, 0.0).astype(BF16)
 
 
-def lane_pick(q):
-    lane = iota((128, 128), 0)
-    i = iota((128, 128), 1)
-    return jnp.where(lane == ((i % 16) // 4) * 32 + q * 4 + i % 4, 1.0, 0.0).astype(BF16)
+def lane_picks():
+    lane = iota((128, 1024), 0)
+    i = iota((128, 1024), 1)
+    return jnp.where(lane == ((i % 16) // 4) * 32 + (i // 128) * 4 + i % 4, 1.0, 0.0).astype(BF16)
 
 
 def lane_put(q):
@@ -76,38 +82,33 @@
     count_ref, ids_hbm, scale_hbm, shift_hbm, gain_hbm, bias_hbm, wcode_hbm, wout_hbm, cot_hbm, obias_hbm,
     emb_ref, gcode_ref, gout_ref, ggain_ref, gbias_ref,
     ids_ref, scale_ref, shift_ref, gain_ref, bias_ref, wcode_ref, wout_ref, cot_ref, obias_ref, s_in,
-    idf, delta, code, pre, gact, dval, act, wown, wout_own, vec, put, mix, nat,
+    idf, delta, code, pre, gact, dval, act, wown, wout_own, vec, put, pick_all, mix, nat, own, share, met,
     st, st2, par, tot, p_send, p_recv, a_send, a_recv,
-    s_id, r_id, s_dl, r_dl, s_st, r_st, s_p, r_p, s_par, r_par, s_st2, r_st2, s_a, r_a, s_tot, r_tot,
+    s_sh, r_sh, s_id, r_id, s_dl, r_dl, s_st, r_st, s_p, r_p, s_par, r_par, s_st2, r_st2, s_a, r_a, s_tot, r_tot,
 ):
     z, x, y, c = (lax.axis_index(a) for a in AXES)
     q = y * 2 + c
     zx = z * 4 + x
 
-    def fold(m):
-        return (m // 2 + m % 2) * (1 - 2 * (m % 2))
-
-    def far(k):
-        tz = lax.rem(z + 4 + fold(k // 4) + 8, 8)
-        tx = lax.rem(x + 2 + fold(k % 4) + 4, 4)
-        return (tz, tx, y, c), tz * 4 + tx
-
-    def near(k):
-        m = k // 2
-        ty = lax.rem(y + m + (m // 2) * (5 - 2 * m), 4)
-        tc = lax.rem(c + k % 2, 2)
-        return (z, x, ty, tc), ty * 2 + tc
+    z_at = [lax.rem(z + d, 8) for d in range(8)]
+    x_at = [lax.rem(x + d, 4) for d in range(4)]
+    x_half = [t // 2 for t in x_at]
+    x_odd = [lax.rem(t, 2) for t in x_at]
+    far = [(z_at[dz], x_at[dx], y, c) for dz, dx in FAR]
+    y_at = [lax.rem(y + d, 4) for d in range(4)]
+    c_at = [c, 1 - c]
+    near = [(z, x, y_at[dy], c_at[dc]) for dy, dc in NEAR]
 
     loads = [
         pltpu.make_async_copy(src, dst, s_in.at[i])
         for i, (src, dst) in enumerate(
             (
                 (ids_hbm, ids_ref),
-                (cot_hbm, cot_ref),
-                (wcode_hbm, wcode_ref),
-                (wout_hbm, wout_ref),
                 (scale_hbm, scale_ref),
                 (shift_hbm, shift_ref),
+                (wcode_hbm, wcode_ref),
+                (cot_hbm, cot_ref),
+                (wout_hbm, wout_ref),
                 (gain_hbm, gain_ref),
                 (bias_hbm, bias_ref),
                 (obias_hbm, obias_ref),
@@ -119,44 +120,25 @@
 
     barrier = pltpu.get_barrier_semaphore()
 
-    def greet_far(k, _):
-        pl.semaphore_signal(barrier, inc=1, device_id=far(k)[0], device_id_type=MESH)
-        return 0
-
-    def greet_near(k, _):
-        pl.semaphore_signal(barrier, inc=1, device_id=near(k)[0], device_id_type=MESH)
-        return 0
-
-    lax.fori_loop(0, PEERS - 1, greet_far, 0)
-    lax.fori_loop(1, GROUP, greet_near, 0)
-
-    def to_near(buf, send, recv):
-        def go(k, _):
-            pltpu.make_async_remote_copy(
-                buf.at[q], buf.at[q], send, recv, device_id=near(k)[0], device_id_type=MESH
-            ).start()
-            return 0
-
-        lax.fori_loop(1, GROUP, go, 0)
-
-    def to_far(buf, send, recv):
-        def go(k, _):
-            pltpu.make_async_remote_copy(
-                buf.at[zx], buf.at[zx], send, recv, device_id=far(k)[0], device_id_type=MESH
-            ).start()
-            return 0
-
-        lax.fori_loop(0, PEERS - 1, go, 0)
-
-    def scatter_far(src, dst, send, recv):
-        def go(k, _):
-            where, t = far(k)
-            pltpu.make_async_remote_copy(
-                src.at[t // 2, lax.rem(t, 2)], dst.at[zx], send, recv, device_id=where, device_id_type=MESH
-            ).start()
-            return 0
-
-        lax.fori_loop(0, PEERS - 1, go, 0)
+    for device in far + near[1:]:
+        pl.semaphore_signal(barrier, inc=1, device_id=device, device_id_type=MESH)
+
+    def send(src, dst, send_sem, recv_sem, device):
+        pltpu.make_async_remote_copy(
+            src, dst, send_sem, recv_sem, device_id=device, device_id_type=MESH
+        ).start()
+
+    def to_near(buf, send_sem, recv_sem):
+        for device in near[1:]:
+            send(buf.at[q], buf.at[q], send_sem, recv_sem, device)
+
+    def to_far(buf, send_sem, recv_sem):
+        for device in far:
+            send(buf.at[zx], buf.at[zx], send_sem, recv_sem, device)
+
+    def scatter_far(src, dst, send_sem, recv_sem):
+        for (dz, dx), device in zip(FAR, far):
+            send(src.at[z_at[dz] * 2 + x_half[dx], x_odd[dx]], dst.at[zx], send_sem, recv_sem, device)
 
     def wait(buf, n, sem):
         part = buf.at[pl.ds(0, n)]
@@ -165,64 +147,98 @@
     count = count_ref[0]
     loads[0].wait()
     slot = iota((2, 128), 0) * 128 + iota((2, 128), 1)
-    idf[q] = jnp.where(slot < count, ids_ref[...].astype(F32), -1.0)
+    idf[0] = jnp.where(slot < count, ids_ref[...].astype(F32), -1.0)
+    for load in loads[1:3]:
+        load.wait()
+    scale = scale_ref[...].astype(F32)
+    high = scale * 256.0
+    high = high - ((high * (1.0 / MODULUS) + MAGIC) - MAGIC) * float(MODULUS)
+    table = []
+    for v in (high, scale, shift_ref[...].astype(F32)):
+        coarse = jnp.floor(v * (1.0 / 256.0)) * 256.0
+        table += [coarse, v - coarse]
+    table = jnp.concatenate(table + [jnp.zeros((10, CODES), F32)], axis=0)
+    flag = jnp.where(iota((16, 128), 0) == 6, 1.0, 0.0)
+    mix[...] = jnp.concatenate([table, flag], axis=1).astype(BF16)
+
+    def hash_rows(k):
+        ident = jnp.concatenate([idf[k, 0:1, :], idf[k, 1:2, :]], axis=1)
+        upper = jnp.floor(ident * (1.0 / 256.0))
+        lower = ident - upper * 256.0
+        alive = jnp.where(ident >= 0.0, 1.0, 0.0)
+        row = iota((16, ROWS), 0)
+        terms = jnp.where(row < 2, upper, jnp.where(row < 4, lower, jnp.where(row < 6, 1.0, jnp.where(row < 7, alive, 0.0))))
+        mixed = dot(terms.astype(BF16), mix[...], TN)
+        value = mixed[:, :CODES]
+        times = (value * (1.0 / MODULUS) + MAGIC) - MAGIC
+        bucket = value - times * float(MODULUS)
+        bucket = jnp.where(bucket < 0.0, bucket + float(MODULUS), bucket)
+        return bucket * (2.0 / (MODULUS - 1)) - 1.0, mixed[:, CODES:]
+
+    def hash_other(k):
+        rows, alive = hash_rows(k)
+        rows = rows.astype(BF16)
+        code[k * ROWS : k * ROWS + ROWS, :] = rows
+        pre[k * ROWS : k * ROWS + ROWS, :] = dot(rows, wown[...]) * alive
+
+    rows, alive = hash_rows(0)
+    rows = (rows * jnp.concatenate([alive] * 4, axis=1)).astype(BF16)
+    code[0:ROWS, :] = rows
+    pick_all[...] = lane_picks()
+    own_z = iota((8, 128), 0) == iota((8, 128), 1) // 16
+    loads[3].wait()
+    rows_of = []
+    for k in range(GROUP):
+        hidden = dot(rows, wcode_ref[:, k * 128 : k * 128 + 128])
+        own[:, k * 128 : k * 128 + 128] = hidden
+        rows_of.append((jnp.sum(hidden, axis=0, keepdims=True), jnp.sum(hidden * hidden, axis=0, keepdims=True)))
+    by_z = jnp.concatenate([r[v] for v in range(2) for r in rows_of], axis=0)
+    by_unit = dot(jnp.concatenate(parts(by_z), axis=0), pick_all[...])
+    by_unit = by_unit[0:16] + by_unit[16:32] + by_unit[32:48]
+    for k in range(GROUP):
+        unit = by_unit[:, k * 128 : k * 128 + 128]
+        share[k] = jnp.concatenate(
+            [jnp.sum(jnp.where(own_z, unit[8 * v : 8 * v + 8], 0.0), axis=0, keepdims=True) for v in range(2)], axis=0
+        )
+
     pl.semaphore_wait(barrier, PEERS - 1 + GROUP - 1)
-    to_near(idf, s_id, r_id.at[q])
-
-    loads[1].wait()
+    for k in range(1, GROUP):
+        dy, dc = NEAR[k]
+        send(share.at[y_at[dy] * 2 + c_at[dc]], met.at[BACK[k]], s_sh, r_sh, near[k])
+    met[0] = share[q]
+    for k in range(1, GROUP):
+        send(idf.at[0], idf.at[BACK[k]], s_id, r_id.at[BACK[k]], near[k])
+
+    loads[4].wait()
     live = iota((ROWS, 128), 0) < count
-    delta[q] = jnp.where(live, cot_ref[...].astype(F32) * (1.0 / 128.0), 0.0).astype(BF16)
-    to_near(delta, s_dl, r_dl)
-
-    for load in loads[2:]:
+    delta[0] = jnp.where(live, cot_ref[...].astype(F32) * (1.0 / 128.0), 0.0).astype(BF16)
+    for k in range(1, GROUP):
+        send(delta.at[0], delta.at[BACK[k]], s_dl, r_dl, near[k])
+
+    for load in loads[5:]:
         load.wait()
     pick = hidden_pick(q)
     wown[...] = dot(wcode_ref[...], pick, NT).astype(BF16)
 
-    scale = scale_ref[...].astype(F32)
-    high = scale * 256.0
-    mix[0:1] = high - ((high * (1.0 / MODULUS) + MAGIC) - MAGIC) * float(MODULUS)
-    mix[1:2] = scale
-    mix[2:3] = shift_ref[...].astype(F32)
-
-    eye = iota((128, 128), 0) == iota((128, 128), 1)
-
-    def hash_rows(qq, carry):
-        total, square = carry
-        pair = idf[qq]
-        ident = jnp.concatenate(
-            [jnp.sum(jnp.where(eye, pair[h : h + 1], 0.0), axis=1, keepdims=True) for h in range(2)], axis=0
-        )
-        upper = jnp.floor(ident * (1.0 / 256.0))
-        lower = ident - upper * 256.0
-        value = mix[0:1] * upper + (mix[1:2] * lower + mix[2:3])
-        times = (value * (1.0 / MODULUS) + MAGIC) - MAGIC
-        bucket = value - times * float(MODULUS)
-        bucket = jnp.where(bucket < 0.0, bucket + float(MODULUS), bucket)
-        rows = (bucket * (2.0 / (MODULUS - 1)) - 1.0).astype(BF16)
-        at = pl.multiple_of(qq * ROWS, ROWS)
-        code[pl.ds(at, ROWS), :] = rows
-        hidden = jnp.where(ident >= 0.0, dot(rows, wown[...]), 0.0)
-        pre[pl.ds(at, ROWS), :] = hidden
-        total = total + jnp.sum(hidden, axis=0, keepdims=True)
-        square = square + jnp.sum(hidden * hidden, axis=0, keepdims=True)
-        return total, square
-
-    def hash_next(k, sums):
-        other = near(k)[1]
-        pltpu.make_async_copy(idf.at[other], idf.at[other], r_id.at[other]).wait()
-        return hash_rows(other, sums)
-
-    zero = jnp.zeros((1, 128), F32)
-    sums = hash_rows(q, (zero, zero))
+    pre[0:ROWS, :] = dot(code[0:ROWS, :], wown[...])
     wout_own[...] = dot(pick, wout_ref[...]).astype(BF16)
-    small = lane_pick(q)
-    own_z = iota((8, 128), 0) == iota((8, 128), 1) // 16
+    small = pick_all[:, pl.ds(pl.multiple_of(q * 128, 128), 128)]
     vec[0:1] = jnp.sum(jnp.where(own_z, exact_pick(gain_ref[...], small), 0.0), axis=0, keepdims=True)
     vec[1:2] = jnp.sum(jnp.where(own_z, exact_pick(bias_ref[...], small), 0.0), axis=0, keepdims=True)
-    sums = lax.fori_loop(1, GROUP, hash_next, sums)
-    st[zx] = jnp.concatenate(sums, axis=0)
+    for b in range(GROUP):
+        put[b * 128 : b * 128 + 128, :] = lane_put(b)
+    pltpu.make_async_copy(idf.at[1], idf.at[1], r_id.at[1]).wait()
+    hash_other(1)
+
+    wait(met, GROUP - 1, r_sh)
+    st[zx] = jnp.sum(met[...], axis=0)
     to_far(st, s_st, r_st)
+
+    for batch in ((2, 3), (4, 5), (6, 7)):
+        for k in batch:
+            pltpu.make_async_copy(idf.at[k], idf.at[k], r_id.at[k]).wait()
+        for k in batch:
+            hash_other(k)
 
     def stacked(full, lo):
         tiles = full.reshape(16, 8, full.shape[1])
@@ -236,17 +252,11 @@
     scatter_far(p_send, p_recv, s_p, r_p)
     alive = jnp.concatenate([jnp.where(idf[b, h : h + 1, :] >= 0.0, 1.0, 0.0) for b in range(8) for h in range(2)], axis=1)
     code_sum = dot(jnp.broadcast_to(alive, (8, GROUP * ROWS)).astype(BF16), code[...])[0:1]
-    for b in range(GROUP):
-        put[b * 128 : b * 128 + 128, :] = lane_put(b)
 
     wait(delta, GROUP - 1, r_dl)
 
-    def back_rows(b, _):
-        at = pl.multiple_of(b * ROWS, ROWS)
-        gact[pl.ds(at, ROWS), :] = dot(delta[b], wout_own[...], NT)
-        return 0
-
-    lax.fori_loop(0, GROUP, back_rows, 0)
+    for k in range(GROUP):
+        gact[k * ROWS : k * ROWS + ROWS, :] = dot(delta[k], wout_own[...], NT)
 
     def in_order(ref):
         blocks = [
@@ -279,6 +289,7 @@
             sum_bias + jnp.sum(d, axis=0, keepdims=True),
         )
 
+    zero = jnp.zeros((1, 128), F32)
     sums = lax.fori_loop(0, GROUP, second, (zero, zero))
     st2[zx] = jnp.concatenate(sums, axis=0)
     to_far(st2, s_st2, r_st2)
@@ -299,16 +310,13 @@
     ordered = in_order(par)
     nat[0] = ordered[0:8]
     nat[1] = ordered[8:16] * gain_ref[...]
-    own_at = pl.multiple_of(q * ROWS, ROWS)
-
-    def embed(k, acc):
-        at = pl.multiple_of(k * 128, 128)
-        hidden = dot(code[pl.ds(own_at, ROWS), :], wcode_ref[:, pl.ds(at, 128)])
-        val = (hidden - nat[0, pl.ds(k, 1), :]) * nat[1, pl.ds(k, 1), :] + bias_ref[pl.ds(k, 1), :]
+
+    acc = jnp.zeros((ROWS, 128), F32)
+    for k in range(GROUP):
+        hidden = own[:, k * 128 : k * 128 + 128]
+        val = (hidden - nat[0, k : k + 1, :]) * nat[1, k : k + 1, :] + bias_ref[k : k + 1, :]
         _, n, r = mish_terms(val)
-        return acc + dot((val * (n * r)).astype(BF16), wout_ref[pl.ds(at, 128), :])
-
-    acc = lax.fori_loop(0, GROUP, embed, jnp.zeros((ROWS, 128), F32))
+        acc = acc + dot((val * (n * r)).astype(BF16), wout_ref[k * 128 : k * 128 + 128, :])
     live = iota((ROWS, 128), 0) < count
     emb_ref[...] = jnp.where(live, acc + obias_ref[...], 0.0).astype(BF16)
 
@@ -342,6 +350,7 @@
     ggain_ref[...] = ordered[0:8]
     gbias_ref[...] = ordered[8:16]
 
+    wait(met, GROUP - 1, s_sh)
     wait(idf, GROUP - 1, s_id)
     wait(delta, GROUP - 1, s_dl)
     wait(st, PEERS - 1, s_st)
@@ -400,8 +409,12 @@
             pltpu.VMEM((128, 128), BF16),
             pltpu.VMEM((8, 128), F32),
             pltpu.VMEM((1024, 128), BF16),
-            pltpu.VMEM((8, CODES), F32),
+            pltpu.VMEM((128, 1024), BF16),
+            pltpu.VMEM((16, CODES + 128), BF16),
             pltpu.VMEM((2, 8, 128), F32),
+            pltpu.VMEM((ROWS, 1024), F32),
+            pltpu.VMEM((GROUP, 2, 128), F32),
+            pltpu.VMEM((GROUP, 2, 128), F32),
             pltpu.VMEM((PEERS, 2, 128), F32),
             pltpu.VMEM((PEERS, 2, 128), F32),
             pltpu.VMEM((GROUP, 2, 128), F32),
@@ -411,7 +424,7 @@
             pltpu.VMEM((16, 2, 8, 384), BF16),
             pltpu.VMEM((PEERS, 8, 384), BF16),
         ]
-        + [dma, dma((GROUP,))]
+        + [dma, dma, dma, dma((GROUP,))]
         + [dma] * 14,
         compiler_params=pltpu.CompilerParams(
             collective_id=0, has_side_effects=True, vmem_limit_bytes=48 << 20

time: 37.9 us -> 34 us (0.90)
  Pallas kernels: 36.5 us -> 32.6 us
    pallas_call x1, Pallas kernels: 35.9 us -> 31.9 us  [per_device(): pl.pallas_call(kernel, out_shape=shapes, in_specs=[pl.BlockSpec(memory_sp...]
where the time goes in v3:
time: 34 us; the launch traced here: 33.9 us
  Pallas kernels  32.6 us (96%)
  between operations  1.29 us (4%)
    pallas_call x1, Pallas kernels, per_device(): pl.pallas_call(kernel, out_shape=shapes, in_specs=[pl.BlockSpec(memory_sp...  31.9 us
    pallas_call x1, Pallas kernels, per_device(): pl.pallas_call(store_kernel, out_shape=shapes, in_specs=[vmem] * 5, out_s...  0.68 us

profile of v3, /device:TPU:1, one launch (start us, length us, event | category | flops | bytes accessed | tf_op | source)
XLA Modules:
  0.0 33.9 jit_solution(6599319468858471159)
XLA Ops:
  1.3 31.9 %shard_map.137 = (bf16[256,128]{1,0:T(8,128)(2,1)S(1)}, f32[4,512]{1,0:T(4,128)S(1)}, f32[4,128]{1,0:T(4,128)S(1)}, f32[8,128]{1,0:T(8,128)S(1)}, f32[8,128]{1,0:T(8,128)S(1)}) custom-call(s32[1]{0:T(128)S(6)} %copy.15.count_ref, s32[2,128]{1,0:T(2,128)} %bitcast.12, s32[1,512]{1,0:T(1,128)} %bitcast.10, s32[1,512]{1,0:T(1,128)} %bitcast.11, ...), custom_call_target="tpu_custom_call" | custom-call | tf_op jit(solution)/shard_map/pallas_call | solution.py:385
  33.2 0.7 %shard_map.138 = (bf16[256,128]{1,0:T(8,128)(2,1)}, f32[4,512]{1,0:T(4,128)}, f32[4,128]{1,0:T(4,128)}, f32[8,128]{1,0:T(8,128)}, f32[8,128]{1,0:T(8,128)}) custom-call(bf16[256,128]{1,0:T(8,128)(2,1)S(1)} %get-tuple-element.15.refs_0_, f32[4,512]{1,0:T(4,128)S(1)} %get-tuple-element.16.refs_1_, f32[4,128]{1,0:T(4,128)S(1)} %get-tuple-element.17.refs_2_, ...), custom_call_target="tpu_custom_call" | custom-call | tf_op jit(solution)/shard_map/pallas_call | solution.py:449

commit v4 on v3

--- a/solution.py
+++ b/solution.py
@@ -83,7 +83,7 @@
     emb_ref, gcode_ref, gout_ref, ggain_ref, gbias_ref,
     ids_ref, scale_ref, shift_ref, gain_ref, bias_ref, wcode_ref, wout_ref, cot_ref, obias_ref, s_in,
     idf, delta, code, pre, gact, dval, act, wown, wout_own, vec, put, pick_all, mix, nat, own, share, met,
-    st, st2, par, tot, p_send, p_recv, a_send, a_recv,
+    st_out, st, st2_own, st2, par, tot, p_send, p_recv, a_send, a_recv,
     s_sh, r_sh, s_id, r_id, s_dl, r_dl, s_st, r_st, s_p, r_p, s_par, r_par, s_st2, r_st2, s_a, r_a, s_tot, r_tot,
 ):
     z, x, y, c = (lax.axis_index(a) for a in AXES)
@@ -95,6 +95,10 @@
     x_half = [t // 2 for t in x_at]
     x_odd = [lax.rem(t, 2) for t in x_at]
     far = [(z_at[dz], x_at[dx], y, c) for dz, dx in FAR]
+    across = [(z_at[dz], x_at[dx], y, 1 - c) for dz, dx in FAR]
+    far_zero = [(z_at[dz], x_at[dx], y, 0) for dz, dx in FAR]
+    far_hub = [(z_at[dz], x_at[dx], y, 1) for dz, dx in FAR]
+    hub = c == 1
     y_at = [lax.rem(y + d, 4) for d in range(4)]
     c_at = [c, 1 - c]
     near = [(z, x, y_at[dy], c_at[dc]) for dy, dc in NEAR]
@@ -120,7 +124,7 @@
 
     barrier = pltpu.get_barrier_semaphore()
 
-    for device in far + near[1:]:
+    for device in far + across + near[1:]:
         pl.semaphore_signal(barrier, inc=1, device_id=device, device_id_type=MESH)
 
     def send(src, dst, send_sem, recv_sem, device):
@@ -131,10 +135,6 @@
     def to_near(buf, send_sem, recv_sem):
         for device in near[1:]:
             send(buf.at[q], buf.at[q], send_sem, recv_sem, device)
-
-    def to_far(buf, send_sem, recv_sem):
-        for device in far:
-            send(buf.at[zx], buf.at[zx], send_sem, recv_sem, device)
 
     def scatter_far(src, dst, send_sem, recv_sem):
         for (dz, dx), device in zip(FAR, far):
@@ -197,15 +197,22 @@
     by_unit = by_unit[0:16] + by_unit[16:32] + by_unit[32:48]
     for k in range(GROUP):
         unit = by_unit[:, k * 128 : k * 128 + 128]
-        share[k] = jnp.concatenate(
+        share[k // 2, k % 2] = jnp.concatenate(
             [jnp.sum(jnp.where(own_z, unit[8 * v : 8 * v + 8], 0.0), axis=0, keepdims=True) for v in range(2)], axis=0
         )
 
-    pl.semaphore_wait(barrier, PEERS - 1 + GROUP - 1)
-    for k in range(1, GROUP):
-        dy, dc = NEAR[k]
-        send(share.at[y_at[dy] * 2 + c_at[dc]], met.at[BACK[k]], s_sh, r_sh, near[k])
-    met[0] = share[q]
+    pl.semaphore_wait(barrier, 2 * (PEERS - 1) + GROUP - 1)
+    for dy in (2, 1, 3):
+        send(share.at[y_at[dy]], met.at[(4 - dy) * 2 + 1 - c], s_sh, r_sh, (z, x, y_at[dy], 1))
+
+    @pl.when(hub)
+    def _():
+        met[0] = share[y]
+
+    @pl.when(c == 0)
+    def _():
+        send(share.at[y], met.at[1], s_sh, r_sh, (z, x, y, 1))
+
     for k in range(1, GROUP):
         send(idf.at[0], idf.at[BACK[k]], s_id, r_id.at[BACK[k]], near[k])
 
@@ -230,9 +237,16 @@
     pltpu.make_async_copy(idf.at[1], idf.at[1], r_id.at[1]).wait()
     hash_other(1)
 
-    wait(met, GROUP - 1, r_sh)
-    st[zx] = jnp.sum(met[...], axis=0)
-    to_far(st, s_st, r_st)
+    @pl.when(hub)
+    def _():
+        wait(met, GROUP - 1, r_sh)
+        both = jnp.sum(met[...], axis=0)
+        st_out[...] = both
+        st[zx] = both[1]
+        for zero, one in zip(far_zero, far_hub):
+            send(st_out.at[0], st.at[zx], s_st, r_st, zero)
+            send(st_out.at[1], st.at[zx], s_st, r_st, one)
+        send(st_out.at[0], st.at[zx], s_st, r_st, (z, x, y, 0))
 
     for batch in ((2, 3), (4, 5), (6, 7)):
         for k in batch:
@@ -258,14 +272,19 @@
     for k in range(GROUP):
         gact[k * ROWS : k * ROWS + ROWS, :] = dot(delta[k], wout_own[...], NT)
 
-    def in_order(ref):
-        blocks = [
-            jnp.concatenate([jnp.where(own_z, ref[b, v : v + 1, :], 0.0) for b in range(GROUP)], axis=1) for v in range(2)
-        ]
+    def in_order(row):
+        blocks = [jnp.concatenate([jnp.where(own_z, row(b, v), 0.0) for b in range(GROUP)], axis=1) for v in range(2)]
         out = dot(jnp.concatenate(parts(jnp.concatenate(blocks, axis=0)), axis=0), put[...])
         return out[0:16] + out[16:32] + out[32:48]
 
-    wait(st, PEERS - 1, r_st)
+    @pl.when(hub)
+    def _():
+        wait(st, PEERS - 1, r_st)
+
+    @pl.when(c == 0)
+    def _():
+        wait(st, PEERS, r_st)
+
     moments = jnp.sum(st[...], axis=0) * (1.0 / TOTAL)
     mean = moments[0:1]
     inv_std = lax.rsqrt(moments[1:2] - mean * mean + EPSILON)
@@ -274,25 +293,39 @@
     par[q] = jnp.concatenate([mean, inv_std], axis=0)
     to_near(par, s_par, r_par)
 
+    slope_in = inv_std * gain
+
     def second(b, carry):
         sum_gain, sum_bias = carry
         at = pl.multiple_of(b * ROWS, ROWS)
-        normed = (pre[pl.ds(at, ROWS), :] - mean) * inv_std
-        val = normed * gain + bias
+        centred = pre[pl.ds(at, ROWS), :] - mean
+        val = centred * slope_in + bias
         u, n, r = mish_terms(val)
-        act[b] = (val * (n * r)).astype(BF16)
-        slope = r * (n + 4.0 * val * (u * (1.0 + u)) * r)
+        ratio = val * r
+        act[b] = (n * ratio).astype(BF16)
+        slope = r * (n + 4.0 * ((n - u) * ratio))
         d = gact[pl.ds(at, ROWS), :] * slope
         dval[pl.ds(at, ROWS), :] = d.astype(BF16)
         return (
-            sum_gain + jnp.sum(d * normed, axis=0, keepdims=True),
+            sum_gain + jnp.sum(d * centred, axis=0, keepdims=True),
             sum_bias + jnp.sum(d, axis=0, keepdims=True),
         )
 
     zero = jnp.zeros((1, 128), F32)
     sums = lax.fori_loop(0, GROUP, second, (zero, zero))
-    st2[zx] = jnp.concatenate(sums, axis=0)
-    to_far(st2, s_st2, r_st2)
+    mine2 = jnp.concatenate([sums[0] * inv_std, sums[1]], axis=0)
+    st2_own[...] = mine2
+    for one in far_hub:
+        send(st2_own, st2.at[c * PEERS + zx], s_st2, r_st2, one)
+
+    @pl.when(hub)
+    def _():
+        st2[PEERS + zx] = mine2
+
+    @pl.when(c == 0)
+    def _():
+        send(st2_own, st2.at[zx], s_st2, r_st2, (z, x, y, 1))
+
 
     a_full = dot(dval[...], code[...], TN)
     o_full = dot(act[...].reshape(GROUP * ROWS, 128), delta[...].reshape(GROUP * ROWS, 128), TN)
@@ -307,7 +340,7 @@
     scatter_far(a_send, a_recv, s_a, r_a)
 
     wait(par, GROUP - 1, r_par)
-    ordered = in_order(par)
+    ordered = in_order(lambda b, v: par[b, v : v + 1, :])
     nat[0] = ordered[0:8]
     nat[1] = ordered[8:16] * gain_ref[...]
 
@@ -316,15 +349,39 @@
         hidden = own[:, k * 128 : k * 128 + 128]
         val = (hidden - nat[0, k : k + 1, :]) * nat[1, k : k + 1, :] + bias_ref[k : k + 1, :]
         _, n, r = mish_terms(val)
-        acc = acc + dot((val * (n * r)).astype(BF16), wout_ref[k * 128 : k * 128 + 128, :])
+        acc = acc + dot((n * (val * r)).astype(BF16), wout_ref[k * 128 : k * 128 + 128, :])
     live = iota((ROWS, 128), 0) < count
     emb_ref[...] = jnp.where(live, acc + obias_ref[...], 0.0).astype(BF16)
 
-    wait(st2, PEERS - 1, r_st2)
-    sums = jnp.sum(st2[...], axis=0)
-    tot[q] = sums
-    to_near(tot, s_tot, r_tot)
-
+    @pl.when(hub)
+    def _():
+        wait(st2, 2 * PEERS - 1, r_st2)
+        for v in range(2):
+            tot[y, v] = jnp.sum(st2[v * PEERS : v * PEERS + PEERS], axis=0)
+        for dy in (2, 1, 3):
+            for core in (0, 1):
+                send(tot.at[y], tot.at[y], s_tot, r_tot, (z, x, y_at[dy], core))
+        send(tot.at[y], tot.at[y], s_tot, r_tot, (z, x, y, 0))
+
+    wait(p_recv, PEERS - 1, r_p)
+    p_sum = jnp.sum(p_recv[...].astype(F32), axis=0)
+    wait(a_recv, PEERS - 1, r_a)
+    a_sum = jnp.sum(a_recv[...].astype(F32), axis=0)
+    gout_ref[...] = a_sum[0:4, 256:384]
+
+    @pl.when(hub)
+    def _():
+        wait(tot, 3, r_tot)
+
+    @pl.when(c == 0)
+    def _():
+        wait(tot, 4, r_tot)
+
+    ordered = in_order(lambda b, v: tot[b // 2, b % 2, v : v + 1, :])
+    ggain_ref[...] = ordered[0:8]
+    gbias_ref[...] = ordered[8:16]
+
+    sums = tot[y, c]
     k1 = inv_std * gain
     k3 = k1 * inv_std * sums[0:1] * (1.0 / TOTAL)
     k2 = k1 * sums[1:2] * (1.0 / TOTAL) - k3 * mean
@@ -333,32 +390,30 @@
     def column(v):
         return jnp.sum(jnp.where(mine, v, 0.0), axis=1, keepdims=True)
 
-    wait(p_recv, PEERS - 1, r_p)
-    p_sum = jnp.sum(p_recv[...].astype(F32), axis=0)
-    wait(a_recv, PEERS - 1, r_a)
-    a_sum = jnp.sum(a_recv[...].astype(F32), axis=0)
     s_all = a_sum[4:8, 256:384]
     upper = jnp.concatenate([s_all[0:1], s_all[1:2]], axis=1)
     lower = jnp.concatenate([s_all[2:3], s_all[3:4]], axis=1)
     s_both = jnp.where(iota((8, 256), 0) < 4, upper, lower)
     grad = column(k1) * a_sum[:, 0:256] - column(k2) * s_both - column(k3) * p_sum
     gcode_ref[...] = jnp.concatenate([grad[0:4], grad[4:8]], axis=1)
-    gout_ref[...] = a_sum[0:4, 256:384]
-
-    wait(tot, GROUP - 1, r_tot)
-    ordered = in_order(tot)
-    ggain_ref[...] = ordered[0:8]
-    gbias_ref[...] = ordered[8:16]
-
-    wait(met, GROUP - 1, s_sh)
+
+    @pl.when(hub)
+    def _():
+        wait(met, 3, s_sh)
+        wait(st2, 2 * PEERS - 1, s_st)
+        wait(st2, PEERS - 1, s_st2)
+        wait(met, GROUP - 1, s_tot)
+
+    @pl.when(c == 0)
+    def _():
+        wait(met, 4, s_sh)
+        wait(st2, PEERS, s_st2)
+
     wait(idf, GROUP - 1, s_id)
     wait(delta, GROUP - 1, s_dl)
-    wait(st, PEERS - 1, s_st)
     wait(p_recv, PEERS - 1, s_p)
     wait(par, GROUP - 1, s_par)
-    wait(st2, PEERS - 1, s_st2)
     wait(a_recv, PEERS - 1, s_a)
-    wait(tot, GROUP - 1, s_tot)
 
 
 def store_kernel(*refs):
@@ -413,12 +468,14 @@
             pltpu.VMEM((16, CODES + 128), BF16),
             pltpu.VMEM((2, 8, 128), F32),
             pltpu.VMEM((ROWS, 1024), F32),
+            pltpu.VMEM((4, 2, 2, 128), F32),
+            pltpu.VMEM((GROUP, 2, 2, 128), F32),
+            pltpu.VMEM((2, 2, 128), F32),
+            pltpu.VMEM((PEERS, 2, 128), F32),
+            pltpu.VMEM((2, 128), F32),
+            pltpu.VMEM((2 * PEERS, 2, 128), F32),
             pltpu.VMEM((GROUP, 2, 128), F32),
-            pltpu.VMEM((GROUP, 2, 128), F32),
-            pltpu.VMEM((PEERS, 2, 128), F32),
-            pltpu.VMEM((PEERS, 2, 128), F32),
-            pltpu.VMEM((GROUP, 2, 128), F32),
-            pltpu.VMEM((GROUP, 2, 128), F32),
+            pltpu.VMEM((4, 2, 2, 128), F32),
             pltpu.VMEM((16, 2, 8, 256), BF16),
             pltpu.VMEM((PEERS, 8, 256), BF16),
             pltpu.VMEM((16, 2, 8, 384), BF16),

time: 34 us -> 32.4 us (0.953)
  Pallas kernels: 32.6 us -> 31 us
    pallas_call x1, Pallas kernels: 31.9 us -> 30.3 us  [per_device(): pl.pallas_call(kernel, out_shape=shapes, in_specs=[pl.BlockSpec(memory_sp...]
where the time goes in v4:
time: 32.4 us; the launch traced here: 32.3 us
  Pallas kernels  31 us (96%)
  between operations  1.29 us (4%)
    pallas_call x1, Pallas kernels, per_device(): pl.pallas_call(kernel, out_shape=shapes, in_specs=[pl.BlockSpec(memory_sp...  30.3 us
    pallas_call x1, Pallas kernels, per_device(): pl.pallas_call(store_kernel, out_shape=shapes, in_specs=[vmem] * 5, out_s...  0.68 us

profile of v4, /device:TPU:1, one launch (start us, length us, event | category | flops | bytes accessed | tf_op | source)
XLA Modules:
  0.0 32.3 jit_solution(6046373882543391165)
XLA Ops:
  1.3 30.3 %shard_map.137 = (bf16[256,128]{1,0:T(8,128)(2,1)S(1)}, f32[4,512]{1,0:T(4,128)S(1)}, f32[4,128]{1,0:T(4,128)S(1)}, f32[8,128]{1,0:T(8,128)S(1)}, f32[8,128]{1,0:T(8,128)S(1)}) custom-call(s32[1]{0:T(128)S(6)} %copy.15.count_ref, s32[2,128]{1,0:T(2,128)} %bitcast.12, s32[1,512]{1,0:T(1,128)} %bitcast.10, s32[1,512]{1,0:T(1,128)} %bitcast.11, ...), custom_call_target="tpu_custom_call" | custom-call | tf_op jit(solution)/shard_map/pallas_call | solution.py:440
  31.6 0.7 %shard_map.138 = (bf16[256,128]{1,0:T(8,128)(2,1)}, f32[4,512]{1,0:T(4,128)}, f32[4,128]{1,0:T(4,128)}, f32[8,128]{1,0:T(8,128)}, f32[8,128]{1,0:T(8,128)}) custom-call(bf16[256,128]{1,0:T(8,128)(2,1)S(1)} %get-tuple-element.15.refs_0_, f32[4,512]{1,0:T(4,128)S(1)} %get-tuple-element.16.refs_1_, f32[4,128]{1,0:T(4,128)S(1)} %get-tuple-element.17.refs_2_, ...), custom_call_target="tpu_custom_call" | custom-call | tf_op jit(solution)/shard_map/pallas_call | solution.py:506

commit v5 on v4

--- a/solution.py
+++ b/solution.py
@@ -25,6 +25,7 @@
     key=lambda o: (-min(o[0], 8 - o[0]) - min(o[1], 4 - o[1]), o),
 )
 NEAR = [(0, 0), (0, 1), (1, 0), (3, 0), (1, 1), (3, 1), (2, 0), (2, 1)]
+ACROSS = {k: NEAR.index((NEAR[k][0], 1)) for k in (2, 3, 6)}
 BACK = [NEAR.index(((4 - dy) % 4, dc)) for dy, dc in NEAR]
 
 NN = (((1,), (0,)), ((), ()))
@@ -84,7 +85,7 @@
     ids_ref, scale_ref, shift_ref, gain_ref, bias_ref, wcode_ref, wout_ref, cot_ref, obias_ref, s_in,
     idf, delta, code, pre, gact, dval, act, wown, wout_own, vec, put, pick_all, mix, nat, own, share, met,
     st_out, st, st2_own, st2, par, tot, p_send, p_recv, a_send, a_recv,
-    s_sh, r_sh, s_id, r_id, s_dl, r_dl, s_st, r_st, s_p, r_p, s_par, r_par, s_st2, r_st2, s_a, r_a, s_tot, r_tot,
+    s_sh, r_sh, s_id, r_id, s_dl, s_df, r_dl, s_st, r_st, s_p, r_p, s_par, r_par, s_st2, r_st2, s_a, r_a, s_tot, r_tot,
 ):
     z, x, y, c = (lax.axis_index(a) for a in AXES)
     q = y * 2 + c
@@ -124,7 +125,7 @@
 
     barrier = pltpu.get_barrier_semaphore()
 
-    for device in far + across + near[1:]:
+    for device in [d for pair in zip(across, far) for d in pair] + near[1:]:
         pl.semaphore_signal(barrier, inc=1, device_id=device, device_id_type=MESH)
 
     def send(src, dst, send_sem, recv_sem, device):
@@ -219,8 +220,8 @@
     loads[4].wait()
     live = iota((ROWS, 128), 0) < count
     delta[0] = jnp.where(live, cot_ref[...].astype(F32) * (1.0 / 128.0), 0.0).astype(BF16)
-    for k in range(1, GROUP):
-        send(delta.at[0], delta.at[BACK[k]], s_dl, r_dl, near[k])
+    for k in (2, 3, 6, 1):
+        send(delta.at[0], delta.at[BACK[k]], s_dl, r_dl.at[BACK[k]], near[k])
 
     for load in loads[5:]:
         load.wait()
@@ -248,28 +249,36 @@
             send(st_out.at[1], st.at[zx], s_st, r_st, one)
         send(st_out.at[0], st.at[zx], s_st, r_st, (z, x, y, 0))
 
-    for batch in ((2, 3), (4, 5), (6, 7)):
+    def arrived(k):
+        pltpu.make_async_copy(delta.at[k], delta.at[k], r_dl.at[k]).wait()
+
+    for batch, passed in (((2, 3), ()), ((4, 5), (2, 3)), ((6, 7), (6,))):
         for k in batch:
             pltpu.make_async_copy(idf.at[k], idf.at[k], r_id.at[k]).wait()
         for k in batch:
             hash_other(k)
-
-    def stacked(full, lo):
-        tiles = full.reshape(16, 8, full.shape[1])
-        part = tiles[:, lo : lo + 4, :]
-        return jnp.concatenate([part[:, :, :256], part[:, :, 256:]], axis=1)
-
-    p_full = dot(pre[...].astype(BF16), code[...], TN)
-    for parity in range(2):
-        p_send[:, parity] = stacked(p_full, parity * 4).astype(BF16)
+        for k in passed:
+            arrived(k)
+            send(delta.at[k], delta.at[ACROSS[k]], s_df, r_dl.at[ACROSS[k]], near[1])
+
+    def pack(buf, full, last):
+        for parity in range(2):
+            lo = parity * 4
+            tiles = full.reshape(16, 8, CODES)[:, lo : lo + 4, :]
+            for b in range(4):
+                buf[:, parity, b] = tiles[:, :, b * 128 : b * 128 + 128].astype(BF16)
+            buf[:, parity, 4] = last[:, lo : lo + 4, :].astype(BF16)
+
+    alive = jnp.concatenate([jnp.where(idf[b, h : h + 1, :] >= 0.0, 1.0, 0.0) for b in range(8) for h in range(2)], axis=1)
+    code_sum = dot(jnp.broadcast_to(alive, (8, GROUP * ROWS)).astype(BF16), code[...])[0:1]
+    s_rows = jnp.concatenate([code_sum[:, 128 * i : 128 * i + 128] for i in range(4)] * 2, axis=0)
+    pack(p_send, dot(pre[...].astype(BF16), code[...], TN), jnp.broadcast_to(s_rows[None], (16, 8, 128)))
     p_recv[zx] = p_send[zx // 2, lax.rem(zx, 2)]
     scatter_far(p_send, p_recv, s_p, r_p)
-    alive = jnp.concatenate([jnp.where(idf[b, h : h + 1, :] >= 0.0, 1.0, 0.0) for b in range(8) for h in range(2)], axis=1)
-    code_sum = dot(jnp.broadcast_to(alive, (8, GROUP * ROWS)).astype(BF16), code[...])[0:1]
-
-    wait(delta, GROUP - 1, r_dl)
 
     for k in range(GROUP):
+        if k in (1, 4, 5, 7):
+            arrived(k)
         gact[k * ROWS : k * ROWS + ROWS, :] = dot(delta[k], wout_own[...], NT)
 
     def in_order(row):
@@ -329,13 +338,7 @@
 
     a_full = dot(dval[...], code[...], TN)
     o_full = dot(act[...].reshape(GROUP * ROWS, 128), delta[...].reshape(GROUP * ROWS, 128), TN)
-    s_rows = jnp.concatenate([code_sum[:, 128 * i : 128 * i + 128] for i in range(4)], axis=0)
-    s_tiles = jnp.broadcast_to(s_rows[None], (16, 4, 128))
-    o_tiles = o_full.reshape(16, 8, 128)
-    for parity in range(2):
-        a_send[:, parity, :, 0:256] = stacked(a_full, parity * 4).astype(BF16)
-        both = jnp.concatenate([o_tiles[:, parity * 4 : parity * 4 + 4, :], s_tiles], axis=1)
-        a_send[:, parity, :, 256:384] = both.astype(BF16)
+    pack(a_send, a_full, o_full.reshape(16, 8, 128))
     a_recv[zx] = a_send[zx // 2, lax.rem(zx, 2)]
     scatter_far(a_send, a_recv, s_a, r_a)
 
@@ -367,7 +370,7 @@
     p_sum = jnp.sum(p_recv[...].astype(F32), axis=0)
     wait(a_recv, PEERS - 1, r_a)
     a_sum = jnp.sum(a_recv[...].astype(F32), axis=0)
-    gout_ref[...] = a_sum[0:4, 256:384]
+    gout_ref[...] = a_sum[4]
 
     @pl.when(hub)
     def _():
@@ -385,17 +388,15 @@
     k1 = inv_std * gain
     k3 = k1 * inv_std * sums[0:1] * (1.0 / TOTAL)
     k2 = k1 * sums[1:2] * (1.0 / TOTAL) - k3 * mean
-    mine = iota((8, 128), 1) == zx * 4 + iota((8, 128), 0) % 4
+    mine = iota((4, 128), 1) == zx * 4 + iota((4, 128), 0)
 
     def column(v):
         return jnp.sum(jnp.where(mine, v, 0.0), axis=1, keepdims=True)
 
-    s_all = a_sum[4:8, 256:384]
-    upper = jnp.concatenate([s_all[0:1], s_all[1:2]], axis=1)
-    lower = jnp.concatenate([s_all[2:3], s_all[3:4]], axis=1)
-    s_both = jnp.where(iota((8, 256), 0) < 4, upper, lower)
-    grad = column(k1) * a_sum[:, 0:256] - column(k2) * s_both - column(k3) * p_sum
-    gcode_ref[...] = jnp.concatenate([grad[0:4], grad[4:8]], axis=1)
+    k1, k2, k3 = column(k1), column(k2), column(k3)
+    gcode_ref[...] = jnp.concatenate(
+        [k1 * a_sum[b] - k2 * p_sum[4, b : b + 1, :] - k3 * p_sum[b] for b in range(4)], axis=1
+    )
 
     @pl.when(hub)
     def _():
@@ -410,7 +411,8 @@
         wait(st2, PEERS, s_st2)
 
     wait(idf, GROUP - 1, s_id)
-    wait(delta, GROUP - 1, s_dl)
+    wait(delta, 4, s_dl)
+    wait(delta, 3, s_df)
     wait(p_recv, PEERS - 1, s_p)
     wait(par, GROUP - 1, s_par)
     wait(a_recv, PEERS - 1, s_a)
@@ -476,13 +478,13 @@
             pltpu.VMEM((2 * PEERS, 2, 128), F32),
             pltpu.VMEM((GROUP, 2, 128), F32),
             pltpu.VMEM((4, 2, 2, 128), F32),
-            pltpu.VMEM((16, 2, 8, 256), BF16),
-            pltpu.VMEM((PEERS, 8, 256), BF16),
-            pltpu.VMEM((16, 2, 8, 384), BF16),
-            pltpu.VMEM((PEERS, 8, 384), BF16),
+            pltpu.VMEM((16, 2, 5, 4, 128), BF16),
+            pltpu.VMEM((PEERS, 5, 4, 128), BF16),
+            pltpu.VMEM((16, 2, 5, 4, 128), BF16),
+            pltpu.VMEM((PEERS, 5, 4, 128), BF16),
         ]
-        + [dma, dma, dma, dma((GROUP,))]
-        + [dma] * 14,
+        + [dma, dma, dma, dma((GROUP,)), dma, dma, dma((GROUP,))]
+        + [dma] * 12,
         compiler_params=pltpu.CompilerParams(
             collective_id=0, has_side_effects=True, vmem_limit_bytes=48 << 20
         ),

time: 32.4 us -> 32.4 us (level)
  no operation moved by 1% of the time
where the time goes in v5:
time: 32.4 us; the launch traced here: 32.3 us
  Pallas kernels  31 us (96%)
  between operations  1.29 us (4%)
    pallas_call x1, Pallas kernels, per_device(): pl.pallas_call(kernel, out_shape=shapes, in_specs=[pl.BlockSpec(memory_sp...  30.3 us
    pallas_call x1, Pallas kernels, per_device(): pl.pallas_call(store_kernel, out_shape=shapes, in_specs=[vmem] * 5, out_s...  0.68 us

profile of v5, /device:TPU:1, one launch (start us, length us, event | category | flops | bytes accessed | tf_op | source)
XLA Modules:
  0.0 32.3 jit_solution(1652947236278204456)
XLA Ops:
  1.3 30.3 %shard_map.137 = (bf16[256,128]{1,0:T(8,128)(2,1)S(1)}, f32[4,512]{1,0:T(4,128)S(1)}, f32[4,128]{1,0:T(4,128)S(1)}, f32[8,128]{1,0:T(8,128)S(1)}, f32[8,128]{1,0:T(8,128)S(1)}) custom-call(s32[1]{0:T(128)S(6)} %copy.15.count_ref, s32[2,128]{1,0:T(2,128)} %bitcast.12, s32[1,512]{1,0:T(1,128)} %bitcast.10, s32[1,512]{1,0:T(1,128)} %bitcast.11, ...), custom_call_target="tpu_custom_call" | custom-call | tf_op jit(solution)/shard_map/pallas_call | solution.py:442
  31.6 0.7 %shard_map.138 = (bf16[256,128]{1,0:T(8,128)(2,1)}, f32[4,512]{1,0:T(4,128)}, f32[4,128]{1,0:T(4,128)}, f32[8,128]{1,0:T(8,128)}, f32[8,128]{1,0:T(8,128)}) custom-call(bf16[256,128]{1,0:T(8,128)(2,1)S(1)} %get-tuple-element.15.refs_0_, f32[4,512]{1,0:T(4,128)S(1)} %get-tuple-element.16.refs_1_, f32[4,128]{1,0:T(4,128)S(1)} %get-tuple-element.17.refs_2_, ...), custom_call_target="tpu_custom_call" | custom-call | tf_op jit(solution)/shard_map/pallas_call | solution.py:508

commit v6 on v5

--- a/solution.py
+++ b/solution.py
@@ -252,7 +252,7 @@
     def arrived(k):
         pltpu.make_async_copy(delta.at[k], delta.at[k], r_dl.at[k]).wait()
 
-    for batch, passed in (((2, 3), ()), ((4, 5), (2, 3)), ((6, 7), (6,))):
+    for batch, passed in (((2, 3, 4, 5, 6, 7), (2, 3, 6)),):
         for k in batch:
             pltpu.make_async_copy(idf.at[k], idf.at[k], r_id.at[k]).wait()
         for k in batch:

time: 32.4 us -> 32.4 us (level)
  no operation moved by 1% of the time
where the time goes in v6:
time: 32.4 us; the launch traced here: 32.2 us
  Pallas kernels  30.9 us (95%)
  between operations  1.29 us (4%)
    pallas_call x1, Pallas kernels, per_device(): pl.pallas_call(kernel, out_shape=shapes, in_specs=[pl.BlockSpec(memory_sp...  30.3 us
    pallas_call x1, Pallas kernels, per_device(): pl.pallas_call(store_kernel, out_shape=shapes, in_specs=[vmem] * 5, out_s...  0.68 us

profile of v6, /device:TPU:1, one launch (start us, length us, event | category | flops | bytes accessed | tf_op | source)
XLA Modules:
  0.0 32.2 jit_solution(11837566251104731143)
XLA Ops:
  1.3 30.3 %shard_map.137 = (bf16[256,128]{1,0:T(8,128)(2,1)S(1)}, f32[4,512]{1,0:T(4,128)S(1)}, f32[4,128]{1,0:T(4,128)S(1)}, f32[8,128]{1,0:T(8,128)S(1)}, f32[8,128]{1,0:T(8,128)S(1)}) custom-call(s32[1]{0:T(128)S(6)} %copy.15.count_ref, s32[2,128]{1,0:T(2,128)} %bitcast.12, s32[1,512]{1,0:T(1,128)} %bitcast.10, s32[1,512]{1,0:T(1,128)} %bitcast.11, ...), custom_call_target="tpu_custom_call" | custom-call | tf_op jit(solution)/shard_map/pallas_call | solution.py:442
  31.5 0.7 %shard_map.138 = (bf16[256,128]{1,0:T(8,128)(2,1)}, f32[4,512]{1,0:T(4,128)}, f32[4,128]{1,0:T(4,128)}, f32[8,128]{1,0:T(8,128)}, f32[8,128]{1,0:T(8,128)}) custom-call(bf16[256,128]{1,0:T(8,128)(2,1)S(1)} %get-tuple-element.15.refs_0_, f32[4,512]{1,0:T(4,128)S(1)} %get-tuple-element.16.refs_1_, f32[4,128]{1,0:T(4,128)S(1)} %get-tuple-element.17.refs_2_, ...), custom_call_target="tpu_custom_call" | custom-call | tf_op jit(solution)/shard_map/pallas_call | solution.py:508
